TPU v7x, 32 devices: a whole 2x2x4 slice. The times are simulated.
32 devices in a mesh: dp: 4 (over z), tensor: 8 (over y, x, core).
Axes of the slice: x: 2, y: 2, z: 4, core: 2. Of those that a mesh axis runs over, the one named last changes fastest.
Arguments:
- activations: bfloat16 [1024, 27648], P('dp', 'tensor'), may hold values from -6 to 6
- left_factor: float32 [216, 216], replicated, may hold values from -2 to 3, as said below
- right_factor: float32 [128, 128], replicated, may hold values from -2 to 3, as said below
- clip_scale: float32 [128, 216], replicated, may hold values from 0.5 to 3
- weight_rows: bfloat16 [27648, 5120], P('tensor'), may hold values from -0.0390625 to 0.0390625
- target: bfloat16 [1024, 5120], P('dp'), may hold values from -6 to 6
Outputs:
- grad_left: float32 [216, 216], replicated
- grad_right: float32 [128, 128], replicated
- grad_input: float32 [1024, 27648], P('dp', 'tensor')
Inputs may be any that keep to these rules, and one draw needn't show every extreme that they name: `left_factor`: the identity plus independent entries of order one over the square root of 216. `right_factor`: the identity plus independent entries of order one over the square root of 128.
All inputs are finite; a program needn't handle non-finite values.
Results may differ from a plain program's by a relative error of at most 0.007.
Values may be sent and summed in bfloat16 or wider, within the bound.
A program may use at most 128 MiB of HBM per device.

v0:
```python
import jax
import jax.numpy as jnp
from jax import lax
from jax.experimental import pallas as pl
from jax.experimental.pallas import tpu as pltpu
from jax.sharding import PartitionSpec as P

BF = jnp.bfloat16
F32 = jnp.float32


def finish_kernel(grad_ref, act_ref, factor_ref, out_ref, left_ref):
    order = factor_ref.shape[0]
    factor = factor_ref[...]

    @pl.when(pl.program_id(0) == 0)
    def _():
        left_ref[...] = jnp.zeros_like(left_ref)

    total = jnp.zeros((order, order), F32)
    for j in range(grad_ref.shape[1] // order):
        here = slice(j * order, (j + 1) * order)
        grad = grad_ref[:, here]
        out_ref[:, here] = lax.dot_general(
            grad, factor, (((1,), (1,)), ((), ())), preferred_element_type=F32
        )
        total = total + lax.dot_general(
            act_ref[:, here], grad, (((0,), (0,)), ((), ())), preferred_element_type=F32
        )
    left_ref[...] += total


def finish(grad, act, factor):
    rows, width = grad.shape
    order = factor.shape[0]
    tile = min(rows, 128)
    return pl.pallas_call(
        finish_kernel,
        grid=(rows // tile,),
        in_specs=[
            pl.BlockSpec((tile, width), lambda i: (i, 0)),
            pl.BlockSpec((tile, width), lambda i: (i, 0)),
            pl.BlockSpec((order, order), lambda i: (0, 0)),
        ],
        out_specs=[
            pl.BlockSpec((tile, width), lambda i: (i, 0)),
            pl.BlockSpec((order, order), lambda i: (0, 0)),
        ],
        out_shape=[
            jax.ShapeDtypeStruct((rows, width), F32),
            jax.ShapeDtypeStruct((order, order), F32),
        ],
        compiler_params=pltpu.CompilerParams(vmem_limit_bytes=48 * 1024 * 1024),
        cost_estimate=pl.CostEstimate(
            flops=4 * rows * width * order, bytes_accessed=8 * rows * width, transcendentals=0
        ),
    )(grad, act, factor.astype(BF))


def split(value):
    head = value.astype(BF)
    return head, (value - head.astype(F32)).astype(BF)


def dot(a, b, dims):
    return lax.dot_general(a, b, ((dims[:1], dims[1:]), ((), ())), preferred_element_type=F32)


def forward_kernel(
    act_ref, left_ref, right_ref, clip_ref, out_ref, mixed_ref, bounded_ref, rows_ref, cols_ref
):
    peers, own, width = act_ref.shape
    order = left_ref.shape[0]
    each = width // order
    left_hi, left_lo = split(left_ref[...])
    right_hi, right_lo = split(right_ref[...])
    clip = clip_ref[...]

    @pl.loop(0, peers)
    def _(s):
        x = jnp.concatenate(
            [act_ref[s, :, j * order : (j + 1) * order] for j in range(each)], axis=0
        )
        mixed = dot(x, left_hi, (1, 0)) + dot(x, left_lo, (1, 0))
        for j in range(each):
            rows_ref[s * each + j] = mixed[j * own : (j + 1) * own]

    @pl.loop(0, own, unroll=4)
    def _(t):
        mixed = rows_ref[:, t, :]
        hi, lo = split(mixed)
        mixed_ref[t] = hi
        rotated = (
            dot(right_hi, hi, (0, 0)) + dot(right_lo, hi, (0, 0)) + dot(right_hi, lo, (0, 0))
        )
        bounded = jnp.tanh(rotated / clip)
        bounded_ref[t] = bounded
        cols_ref[:, t, :] = clip * bounded

    @pl.loop(0, peers)
    def _(s):
        for j in range(each):
            out_ref[s, :, j * order : (j + 1) * order] = cols_ref[s * each + j].astype(BF)


def backward_kernel(
    grad_ref, mixed_ref, bounded_ref, right_ref, out_ref, sum_ref, rows_ref, cols_ref
):
    peers, own, width = grad_ref.shape
    order = bounded_ref.shape[2]
    each = width // order
    right = right_ref[...].astype(BF)

    @pl.loop(0, peers)
    def _(s):
        for j in range(each):
            rows_ref[s * each + j] = grad_ref[s, :, j * order : (j + 1) * order].astype(F32)

    sum_ref[...] = jnp.zeros_like(sum_ref)

    @pl.loop(0, own, unroll=4)
    def _(t):
        bounded = bounded_ref[t]
        rotated_grad = (rows_ref[:, t, :] * (1.0 - bounded * bounded)).astype(BF)
        sum_ref[...] += dot(mixed_ref[t], rotated_grad, (1, 1))
        cols_ref[:, t, :] = dot(right, rotated_grad, (1, 0))

    @pl.loop(0, peers)
    def _(s):
        for j in range(each):
            out_ref[s, :, j * order : (j + 1) * order] = cols_ref[s * each + j].astype(BF)


def owner_call(kernel, outs, scratch, *args):
    return pl.pallas_call(
        kernel,
        out_shape=[jax.ShapeDtypeStruct(*out) for out in outs],
        in_specs=[pl.BlockSpec(memory_space=pltpu.VMEM)] * len(args),
        out_specs=[pl.BlockSpec(memory_space=pltpu.VMEM)] * len(outs),
        scratch_shapes=[pltpu.VMEM(scratch, F32)] * 2,
        compiler_params=pltpu.CompilerParams(vmem_limit_bytes=56 * 1024 * 1024),
    )(*args)


def local(activations, left_factor, right_factor, clip_scale, weight_rows, target):
    peers = lax.axis_size("tensor")
    everyone = lax.axis_size("dp") * peers
    tok_rows, width = activations.shape
    width_left = left_factor.shape[0]
    width_right = right_factor.shape[0]
    own = tok_rows // peers

    def exchange(blocks):
        got = lax.all_to_all(
            blocks.reshape(tok_rows, width), "tensor", split_axis=0, concat_axis=0, tiled=True
        )
        return got.reshape(peers, own, width)

    flat = (peers, own, width)
    cube = (own, width_right, width_left)
    by_row = (width_right, own, width_left)
    clipped, mixed, bounded = owner_call(
        forward_kernel, [(flat, BF), (cube, BF), (cube, F32)], by_row,
        exchange(activations), left_factor, right_factor, clip_scale,
    )
    clipped = exchange(clipped).reshape(tok_rows, width)
    partial_out = jnp.dot(clipped, weight_rows, preferred_element_type=F32).astype(BF)
    chips = peers // 2
    core = lax.axis_index("tensor") % 2
    same_core = [[2 * q + c for q in range(chips)] for c in range(2)]
    swap = [(d, d ^ 1) for d in range(peers)]
    blocks = partial_out.reshape(chips, 2, own, -1)
    there = lax.dynamic_index_in_dim(blocks, 1 - core, 1, keepdims=False)
    here = lax.dynamic_index_in_dim(blocks, core, 1, keepdims=False)
    there = lax.ppermute(there, "tensor", swap)
    paired = (here.astype(F32) + there.astype(F32)).astype(BF)
    terms = lax.all_to_all(
        paired, "tensor", split_axis=0, concat_axis=0, axis_index_groups=same_core, tiled=True
    )
    total = jnp.sum(terms.astype(F32), axis=0)
    mine = lax.dynamic_slice_in_dim(target, lax.axis_index("tensor") * own, own, 0)
    mine = (total - mine.astype(F32)).astype(BF)
    got = lax.all_to_all(
        jnp.broadcast_to(mine[None], (chips, *mine.shape)),
        "tensor", split_axis=0, concat_axis=0, axis_index_groups=same_core, tiled=True,
    )
    other = lax.ppermute(got, "tensor", swap)
    first = jnp.where(core == 0, got, other)
    second = jnp.where(core == 0, other, got)
    out_grad = jnp.stack([first, second], axis=1).reshape(tok_rows, -1)
    clipped_grad = lax.dot_general(
        out_grad, weight_rows, (((1,), (1,)), ((), ())), preferred_element_type=F32
    ).astype(BF)
    mixed_grad, right_part = owner_call(
        backward_kernel, [(flat, BF), ((width_right, width_right), F32)], by_row,
        exchange(clipped_grad), mixed, bounded, right_factor,
    )
    grad_back = exchange(mixed_grad).reshape(tok_rows, width)
    input_grad, left_part = finish(grad_back, activations, left_factor)

    cols = max(width_left, width_right)
    stacked = jnp.concatenate(
        [
            jnp.pad(left_part, ((0, 0), (0, cols - width_left))),
            jnp.pad(right_part, ((0, 0), (0, cols - width_right))),
        ],
        axis=0,
    )
    rows = -(-stacked.shape[0] // (8 * peers)) * 8
    stacked = jnp.pad(stacked, ((0, rows * peers - stacked.shape[0]), (0, 0)))

    def spread(piece, axis, times):
        copies = jnp.broadcast_to(piece[None], (times, *piece.shape))
        return lax.all_to_all(copies, axis, split_axis=0, concat_axis=0, tiled=True)

    shares = lax.all_to_all(
        stacked.reshape(peers, rows, cols), "tensor", split_axis=0, concat_axis=0, tiled=True
    )
    share = jnp.sum(spread(jnp.sum(shares, axis=0), "dp", lax.axis_size("dp")), axis=0)
    sums = spread(share, "tensor", peers).reshape(rows * peers, cols)
    left_sum = sums[:width_left, :width_left]
    right_sum = sums[width_left : width_left + width_right, :width_right]
    return (left_sum, right_sum, input_grad)


def solution(mesh):
    placed = (P("dp", "tensor"), P(), P(), P(), P("tensor", None), P("dp", None))
    return jax.shard_map(
        local, mesh=mesh, in_specs=placed, out_specs=(P(), P(), P("dp", "tensor")), check_vma=False
    )
```

profile of v0, /device:TPU:0, one launch (start us, length us, event | category | flops | bytes accessed | tf_op | source)
XLA Modules:
  0.0 279.2 jit_solution(11222155936612393815)
XLA Ops:
  0.6 0.0 copy-start.4
  0.6 5.3 %all-to-all-start = ((bf16[8,32,3456]{2,1,0:T(8,128)(2,1)}), bf16[8,32,3456]{2,1,0:T(8,128)(2,1)S(1)}, u32[]{:S(2)}, u32[]{:S(2)}) async-start(bf16[8,32,3456]{2,1,0:T(8,128)(2,1)} %bitcast.23), calls=%async_computation | async-start | bytes 3538944 | tf_op jit(solution)/shard_map/all_to_all | solution.py:154
  6.0 0.0 copy-done.4
  6.0 0.8 copy.12.clip_ref
  6.7 22.3 %all-to-all-done.act_ref = bf16[8,32,3456]{2,1,0:T(8,128)(2,1)S(1)} async-done(((bf16[8,32,3456]{2,1,0:T(8,128)(2,1)}), bf16[8,32,3456]{2,1,0:T(8,128)(2,1)S(1)}, u32[]{:S(2)}, u32[]{:S(2)}) %all-to-all-start) | async-done | bytes 1769504 | tf_op jit(solution)/shard_map/all_to_all | solution.py:154
  29.1 0.0 copy-start.2
  29.1 1.2 copy-done.2
  30.3 25.3 %shard_map.85 = (bf16[8,32,3456]{2,1,0:T(8,128)(2,1)}, bf16[32,128,216]{2,1,0:T(8,128)(2,1)}, f32[32,128,216]{2,1,0:T(8,128)}) custom-call(bf16[8,32,3456]{2,1,0:T(8,128)(2,1)} %copy-done.2, f32[216,216]{1,0:T(8,128)} %left_ref.1, f32[128,128]{1,0:T(8,128)} %right_ref.3, f32[128,216]{1,0:T(8,128)} %copy.12.clip_ref), custom_call_target="tpu_custom_call" | custom-call | tf_op jit(solution)/shard_map/pallas_call | solution.py:135
  55.6 3.6 %all-to-all-start.1 = ((bf16[8,32,3456]{2,1,0:T(8,128)(2,1)}), bf16[8,32,3456]{2,1,0:T(8,128)(2,1)S(1)}, u32[]{:S(2)}, u32[]{:S(2)}) async-start(bf16[8,32,3456]{2,1,0:T(8,128)(2,1)} %get-tuple-element.10), calls=%async_computation.1 | async-start | bytes 3538944 | tf_op jit(solution)/shard_map/all_to_all | solution.py:154
  59.2 23.0 %all-to-all-done.1 = bf16[8,32,3456]{2,1,0:T(8,128)(2,1)S(1)} async-done(((bf16[8,32,3456]{2,1,0:T(8,128)(2,1)}), bf16[8,32,3456]{2,1,0:T(8,128)(2,1)S(1)}, u32[]{:S(2)}, u32[]{:S(2)}) %all-to-all-start.1) | async-done | bytes 1769504 | tf_op jit(solution)/shard_map/all_to_all | solution.py:154
  82.2 0.0 copy-start.3
  82.2 1.2 copy-done.3
  83.5 16.5 %convolution_convert_fusion = bf16[256,5120]{1,0:T(8,128)(2,1)S(1)} fusion(bf16[256,3456]{1,0:T(8,128)(2,1)} %bitcast.28, bf16[3456,5120]{1,0:T(8,128)(2,1)} %param.10), kind=kOutput, calls=%fused_computation | convolution fusion | flops 9061007360 | bytes 39780352 | tf_op jit(solution)/shard_map/dot_general | solution.py:167
  100.0 1.2 dynamic-slice_bitcast_fusion
  101.2 0.0 collective-permute-start
  101.2 3.4 %collective-permute-done = bf16[4,32,5120]{2,1,0:T(8,128)(2,1)} collective-permute-done((bf16[4,32,5120]{2,1,0:T(8,128)(2,1)}, bf16[4,32,5120]{2,1,0:T(8,128)(2,1)}, u32[]{:S(2)}, u32[]{:S(2)}) %collective-permute-start) | collective-permute-done | bytes 1310752 | tf_op jit(solution)/shard_map/ppermute | solution.py:175
  104.5 2.7 fusion
  107.2 3.5 %all-to-all-start.2 = ((bf16[4,32,5120]{2,1,0:T(8,128)(2,1)}), bf16[4,32,5120]{2,1,0:T(8,128)(2,1)S(1)}, u32[]{:S(2)}, u32[]{:S(2)}) async-start(bf16[4,32,5120]{2,1,0:T(8,128)(2,1)} %fusion), calls=%async_computation.2 | async-start | bytes 2621440 | tf_op jit(solution)/shard_map/all_to_all | solution.py:177
  110.8 17.0 %all-to-all-done.2 = bf16[4,32,5120]{2,1,0:T(8,128)(2,1)S(1)} async-done(((bf16[4,32,5120]{2,1,0:T(8,128)(2,1)}), bf16[4,32,5120]{2,1,0:T(8,128)(2,1)S(1)}, u32[]{:S(2)}, u32[]{:S(2)}) %all-to-all-start.2) | async-done | bytes 1310752 | tf_op jit(solution)/shard_map/all_to_all | solution.py:177
  127.8 0.2 convert_reduce_fusion
  128.0 1.1 subtract_convert_fusion
  129.0 0.1 broadcast_in_dim.6
  129.1 19.1 %all_to_all.60 = bf16[4,32,5120]{2,1,0:T(8,128)(2,1)S(1)} all-to-all(bf16[4,32,5120]{2,1,0:T(8,128)(2,1)S(1)} %broadcast_in_dim.6), channel_id=1, replica_groups={{0,2,4,6},{1,3,5,7},{8,10,12,14},{9,11,13,15},{16,18,20,22},{17,19,21,2..., dimensions={0} | all-to-all | bytes 2621440 | tf_op jit(solution)/shard_map/all_to_all | solution.py:183
  148.3 0.0 collective-permute-start.1
  148.3 3.0 %collective-permute-done.1 = bf16[4,32,5120]{2,1,0:T(8,128)(2,1)S(1)} collective-permute-done((bf16[4,32,5120]{2,1,0:T(8,128)(2,1)S(1)}, bf16[4,32,5120]{2,1,0:T(8,128)(2,1)S(1)}, u32[]{:S(2)}, u32[]{:S(2)}) %collective-permute-start.1) | collective-permute-done | bytes 1310752 | tf_op jit(solution)/shard_map/ppermute | solution.py:187
  151.3 0.2 select_bitcast_fusion.1
  151.5 0.2 pad_maximum_fusion
  151.7 16.4 %convolution_convert_fusion.1 = bf16[256,3456]{1,0:T(8,128)(2,1)} fusion(bf16[256,5120]{1,0:T(8,128)(2,1)S(1)} %bitcast.27, bf16[3456,5120]{1,0:T(8,128)(2,1)} %param.10), kind=kOutput, calls=%fused_computation.1 | convolution fusion | flops 9060581376 | bytes 39780352 | tf_op jit(solution)/shard_map/dot_general | solution.py:191
  168.1 27.4 %all_to_all.61.grad_ref = bf16[8,32,3456]{2,1,0:T(8,128)(2,1)} all-to-all(bf16[8,32,3456]{2,1,0:T(8,128)(2,1)} %bitcast.29), channel_id=1, replica_groups=mesh['dp'=4,'tensor'=8] {'tensor'}, dimensions={0} | all-to-all | bytes 3538944 | tf_op jit(solution)/shard_map/all_to_all | solution.py:154
  195.5 12.2 %shard_map.86 = (bf16[8,32,3456]{2,1,0:T(8,128)(2,1)}, f32[128,128]{1,0:T(8,128)}) custom-call(bf16[8,32,3456]{2,1,0:T(8,128)(2,1)} %all_to_all.61.grad_ref, bf16[32,128,216]{2,1,0:T(8,128)(2,1)} %get-tuple-element.11.mixed_ref, f32[32,128,216]{2,1,0:T(8,128)} %get-tuple-element.12.bounded_ref, f32[128,128]{1,0:T(8,128)} %right_ref.3), custom_call_target="tpu_custom_call" | custom-call | tf_op jit(solution)/shard_map/pallas_call | solution.py:135
  207.7 0.0 copy-start
  207.7 3.9 %all-to-all-start.5 = ((bf16[8,32,3456]{2,1,0:T(8,128)(2,1)}), bf16[8,32,3456]{2,1,0:T(8,128)(2,1)S(1)}, u32[]{:S(2)}, u32[]{:S(2)}) async-start(bf16[8,32,3456]{2,1,0:T(8,128)(2,1)} %get-tuple-element.13), calls=%async_computation.5 | async-start | bytes 3538944 | tf_op jit(solution)/shard_map/all_to_all | solution.py:154
  211.6 1.6 convert_element_type.43.factor_ref
  213.2 21.3 %all-to-all-done.5 = bf16[8,32,3456]{2,1,0:T(8,128)(2,1)S(1)} async-done(((bf16[8,32,3456]{2,1,0:T(8,128)(2,1)}), bf16[8,32,3456]{2,1,0:T(8,128)(2,1)S(1)}, u32[]{:S(2)}, u32[]{:S(2)}) %all-to-all-start.5) | async-done | bytes 1769504 | tf_op jit(solution)/shard_map/all_to_all | solution.py:154
  234.5 0.0 copy-done
  234.5 0.0 copy-start.1
  234.5 0.9 copy-done.1
  235.4 0.0 copy-start.5
  235.4 8.9 %shard_map.87 = (f32[256,3456]{1,0:T(8,128)}, f32[216,216]{1,0:T(8,128)S(1)}) custom-call(bf16[256,3456]{1,0:T(8,128)(2,1)S(1)} %bitcast.24, bf16[256,3456]{1,0:T(8,128)(2,1)S(1)} %copy-done, bf16[216,216]{1,0:T(8,128)(2,1)S(1)} %copy-done.1), custom_call_target="tpu_custom_call" | custom-call | flops 764411904 | bytes 7077888 | tf_op jit(solution)/shard_map/pallas_call | solution.py:37
  244.2 0.0 copy-done.5
  244.3 10.7 %all_to_all.62 = f32[8,48,216]{2,1,0:T(8,128)S(1)} all-to-all(f32[8,48,216]{2,1,0:T(8,128)S(1)} %bitcast.30), channel_id=1, replica_groups=mesh['dp'=4,'tensor'=8] {'tensor'}, dimensions={0} | all-to-all | bytes 663552 | tf_op jit(solution)/shard_map/all_to_all | solution.py:216
  255.0 12.0 %all_to_all.63 = f32[4,48,216]{2,1,0:T(8,128)S(1)} all-to-all(f32[4,48,216]{2,1,0:T(8,128)S(1)} %broadcast_in_dim.7), channel_id=1, replica_groups=mesh['dp'=4,'tensor'=8] {'dp'}, dimensions={0} | all-to-all | bytes 331776 | tf_op jit(solution)/shard_map/all_to_all | solution.py:214
  267.2 10.7 %all_to_all.64 = f32[8,48,216]{2,1,0:T(8,128)S(1)} all-to-all(f32[8,48,216]{2,1,0:T(8,128)S(1)} %broadcast_in_dim.8), channel_id=1, replica_groups=mesh['dp'=4,'tensor'=8] {'tensor'}, dimensions={0} | all-to-all | bytes 663552 | tf_op jit(solution)/shard_map/all_to_all | solution.py:214
  277.9 0.7 slice.8
  278.6 0.6 slice.9
  (6 shorter events, 0.1 us)
Async XLA Ops:
  0.6 5.4 %copy-start.4 = (f32[128,216]{0,1:T(8,128)S(1)}, f32[128,216]{0,1:T(8,128)}, u32[]{:S(2)}) copy-start(f32[128,216]{0,1:T(8,128)} %param.9) | copy-start | bytes 331780
  0.6 28.4 %all-to-all-start = ((bf16[8,32,3456]{2,1,0:T(8,128)(2,1)}), bf16[8,32,3456]{2,1,0:T(8,128)(2,1)S(1)}, u32[]{:S(2)}, u32[]{:S(2)}) async-start(bf16[8,32,3456]{2,1,0:T(8,128)(2,1)} %bitcast.23), calls=%async_computation | async-start | bytes 3538944 | tf_op jit(solution)/shard_map/all_to_all | solution.py:154
  29.1 1.2 copy-start.2
  55.6 26.6 %all-to-all-start.1 = ((bf16[8,32,3456]{2,1,0:T(8,128)(2,1)}), bf16[8,32,3456]{2,1,0:T(8,128)(2,1)S(1)}, u32[]{:S(2)}, u32[]{:S(2)}) async-start(bf16[8,32,3456]{2,1,0:T(8,128)(2,1)} %get-tuple-element.10), calls=%async_computation.1 | async-start | bytes 3538944 | tf_op jit(solution)/shard_map/all_to_all | solution.py:154
  82.2 1.2 copy-start.3
  101.2 3.4 %collective-permute-start = (bf16[4,32,5120]{2,1,0:T(8,128)(2,1)}, bf16[4,32,5120]{2,1,0:T(8,128)(2,1)}, u32[]{:S(2)}, u32[]{:S(2)}) collective-permute-start(bf16[4,32,5120]{2,1,0:T(8,128)(2,1)} %dynamic-slice_bitcast_fusion), channel_id=1, source_target_pairs={{0,1},{1,0},{2,3},{3,2},{4,5},{5,4},{6,7},{7,6},{8,9},{9,8},{10,11... | collective-permute-start | bytes 3932168 | tf_op jit(solution)/shard_map/ppermute | solution.py:175
  107.2 20.5 %all-to-all-start.2 = ((bf16[4,32,5120]{2,1,0:T(8,128)(2,1)}), bf16[4,32,5120]{2,1,0:T(8,128)(2,1)S(1)}, u32[]{:S(2)}, u32[]{:S(2)}) async-start(bf16[4,32,5120]{2,1,0:T(8,128)(2,1)} %fusion), calls=%async_computation.2 | async-start | bytes 2621440 | tf_op jit(solution)/shard_map/all_to_all | solution.py:177
  148.3 3.0 %collective-permute-start.1 = (bf16[4,32,5120]{2,1,0:T(8,128)(2,1)S(1)}, bf16[4,32,5120]{2,1,0:T(8,128)(2,1)S(1)}, u32[]{:S(2)}, u32[]{:S(2)}) collective-permute-start(bf16[4,32,5120]{2,1,0:T(8,128)(2,1)S(1)} %all_to_all.60), channel_id=1, source_target_pairs={{0,1},{1,0},{2,3},{3,2},{4,5},{5,4},{6,7},{7,6},{8,9},{9,8},{10,11... | collective-permute-start | bytes 3932168 | tf_op jit(solution)/shard_map/ppermute | solution.py:187
  207.7 26.8 %copy-start = (bf16[256,3456]{1,0:T(8,128)(2,1)S(1)}, bf16[256,3456]{1,0:T(8,128)(2,1)}, u32[]{:S(2)}) copy-start(bf16[256,3456]{1,0:T(8,128)(2,1)} %act_ref.1) | copy-start | bytes 5308420
  207.7 26.8 %all-to-all-start.5 = ((bf16[8,32,3456]{2,1,0:T(8,128)(2,1)}), bf16[8,32,3456]{2,1,0:T(8,128)(2,1)S(1)}, u32[]{:S(2)}, u32[]{:S(2)}) async-start(bf16[8,32,3456]{2,1,0:T(8,128)(2,1)} %get-tuple-element.13), calls=%async_computation.5 | async-start | bytes 3538944 | tf_op jit(solution)/shard_map/all_to_all | solution.py:154
  234.5 0.9 copy-start.1
  235.4 8.9 %copy-start.5 = (f32[128,128]{1,0:T(8,128)S(1)}, f32[128,128]{1,0:T(8,128)}, u32[]{:S(2)}) copy-start(f32[128,128]{1,0:T(8,128)} %get-tuple-element.15) | copy-start | bytes 196612
where the time goes:
time: 280 us; the launch traced here: 279 us
  waiting for transfers between devices  90 us (32%)
  blocking collectives  79.9 us (29%)
  Pallas kernels  46.4 us (17%)
  matrix products  32.9 us (12%)
  starting transfers between devices  16.4 us (6%)
  local copies, waits for them, and re-layouts  6.86 us (2%)
  other arithmetic  6.02 us (2%)
    all_to_all x3, waiting for transfers between devices, exchange(): lax.all_to_all(blocks.reshape(tok_rows, width), 'tensor', split_axis=0, c...  66.6 us
    pallas_call x2, Pallas kernels, owner_call(): pl.pallas_call(kernel, out_shape=[jax.ShapeDtypeStruct(*out) for out in o...  37.5 us
    all_to_all x1, blocking collectives, exchange(): lax.all_to_all(blocks.reshape(tok_rows, width), 'tensor', split_axis=0, c...  27.4 us
    all_to_all x2, blocking collectives, spread(): return lax.all_to_all(copies, axis, split_axis=0, concat_axis=0, tiled=True)  22.8 us
    all_to_all x1, blocking collectives, local(): lax.all_to_all(jnp.broadcast_to(mine[None], (chips, *mine.shape)), 'tenso...  19.1 us
    all_to_all x1, waiting for transfers between devices, local(): lax.all_to_all(paired, 'tensor', split_axis=0, concat_axis=0, axis_index_...  17 us
    dot_general x1, matrix products, local(): jnp.dot(clipped, weight_rows, preferred_element_type=F32).astype(BF)  16.5 us
    dot_general x1, matrix products, local(): lax.dot_general(out_grad, weight_rows, (((1,), (1,)), ((), ())), preferre...  16.4 us
  transfers between devices with their start and end apart: 6, of which 6 were waited for; matrix products, arithmetic and copies ran while one was open for 1% of the time, Pallas kernels for 0%

commit v1 on v0

--- a/solution.py
+++ b/solution.py
@@ -66,41 +66,146 @@
     return lax.dot_general(a, b, ((dims[:1], dims[1:]), ((), ())), preferred_element_type=F32)
 
 
+MESH = pl.DeviceIdType.MESH
+
+
+def greet(peers, me):
+    barrier = pltpu.get_barrier_semaphore()
+
+    @pl.loop(1, peers)
+    def _(o):
+        pl.semaphore_signal(
+            barrier, inc=1, device_id={"tensor": lax.rem(me + o, peers)}, device_id_type=MESH
+        )
+
+    pl.semaphore_wait(barrier, peers - 1)
+
+
+def to_peer(src, dst, send, recv, peer):
+    return pltpu.make_async_remote_copy(
+        src_ref=src, dst_ref=dst, send_sem=send, recv_sem=recv,
+        device_id={"tensor": peer}, device_id_type=MESH,
+    )
+
+
 def forward_kernel(
-    act_ref, left_ref, right_ref, clip_ref, out_ref, mixed_ref, bounded_ref, rows_ref, cols_ref
+    act_ref, left_ref, right_ref, clip_ref,
+    out_ref, mixed_ref, bounded_ref,
+    in_ref, done_ref, rows_ref, cols_ref,
+    in_send, in_recv, out_send, out_recv, own_in, own_out,
 ):
-    peers, own, width = act_ref.shape
+    peers, chunks, rows, width = act_ref.shape
     order = left_ref.shape[0]
     each = width // order
+    me = lax.axis_index("tensor")
+    greet(peers, me)
+
+    @pl.loop(0, chunks)
+    def _(c):
+        pltpu.make_async_copy(act_ref.at[me, c], in_ref.at[me, c], own_in.at[c]).start()
+
+        @pl.loop(1, peers)
+        def _(o):
+            p = lax.rem(me + o, peers)
+            to_peer(
+                act_ref.at[p, c], in_ref.at[me, c], in_send.at[c, p], in_recv.at[c, me], p
+            ).start()
+
     left_hi, left_lo = split(left_ref[...])
     right_hi, right_lo = split(right_ref[...])
     clip = clip_ref[...]
 
-    @pl.loop(0, peers)
-    def _(s):
-        x = jnp.concatenate(
-            [act_ref[s, :, j * order : (j + 1) * order] for j in range(each)], axis=0
-        )
-        mixed = dot(x, left_hi, (1, 0)) + dot(x, left_lo, (1, 0))
-        for j in range(each):
-            rows_ref[s * each + j] = mixed[j * own : (j + 1) * own]
-
-    @pl.loop(0, own, unroll=4)
-    def _(t):
-        mixed = rows_ref[:, t, :]
-        hi, lo = split(mixed)
-        mixed_ref[t] = hi
-        rotated = (
-            dot(right_hi, hi, (0, 0)) + dot(right_lo, hi, (0, 0)) + dot(right_hi, lo, (0, 0))
-        )
-        bounded = jnp.tanh(rotated / clip)
-        bounded_ref[t] = bounded
-        cols_ref[:, t, :] = clip * bounded
-
-    @pl.loop(0, peers)
-    def _(s):
-        for j in range(each):
-            out_ref[s, :, j * order : (j + 1) * order] = cols_ref[s * each + j].astype(BF)
+    @pl.loop(0, chunks)
+    def _(c):
+        pltpu.make_async_copy(act_ref.at[me, c], in_ref.at[me, c], own_in.at[c]).wait()
+
+        @pl.loop(1, peers)
+        def _(o):
+            s = lax.rem(me + o, peers)
+            to_peer(
+                act_ref.at[s, c], in_ref.at[s, c], in_send.at[c, s], in_recv.at[c, s], s
+            ).wait_recv()
+
+        @pl.loop(0, peers)
+        def _(s):
+            x = jnp.concatenate(
+                [in_ref[s, c, :, j * order : (j + 1) * order] for j in range(each)], axis=0
+            )
+            mixed = dot(x, left_hi, (1, 0)) + dot(x, left_lo, (1, 0))
+            for j in range(each):
+                rows_ref[s * each + j] = mixed[j * rows : (j + 1) * rows]
+
+        @pl.loop(0, rows, unroll=4)
+        def _(t):
+            mixed = rows_ref[:, t, :]
+            hi, lo = split(mixed)
+            mixed_ref[c * rows + t] = hi
+            rotated = (
+                dot(right_hi, hi, (0, 0)) + dot(right_lo, hi, (0, 0)) + dot(right_hi, lo, (0, 0))
+            )
+            bounded = jnp.tanh(rotated / clip)
+            bounded_ref[c * rows + t] = bounded
+            cols_ref[:, t, :] = clip * bounded
+
+        @pl.loop(0, peers)
+        def _(s):
+            for j in range(each):
+                done_ref[s, c, :, j * order : (j + 1) * order] = cols_ref[s * each + j].astype(BF)
+
+        pltpu.make_async_copy(done_ref.at[me, c], out_ref.at[me, c], own_out.at[c]).start()
+
+        @pl.loop(1, peers)
+        def _(o):
+            p = lax.rem(me + o, peers)
+            to_peer(
+                done_ref.at[p, c], out_ref.at[me, c], out_send.at[c, p], out_recv.at[c, me], p
+            ).start()
+
+    @pl.loop(0, chunks)
+    def _(c):
+        pltpu.make_async_copy(done_ref.at[me, c], out_ref.at[me, c], own_out.at[c]).wait()
+
+        @pl.loop(1, peers)
+        def _(o):
+            p = lax.rem(me + o, peers)
+            to_peer(
+                act_ref.at[p, c], in_ref.at[me, c], in_send.at[c, p], in_recv.at[c, p], p
+            ).wait_send()
+            to_peer(
+                done_ref.at[p, c], out_ref.at[p, c], out_send.at[c, p], out_recv.at[c, p], p
+            ).wait()
+
+
+def forward(act, left, right, clip, rows):
+    tok_rows, width = act.shape
+    peers = lax.axis_size("tensor")
+    own = tok_rows // peers
+    chunks = own // rows
+    order, side = left.shape[0], right.shape[0]
+    blocks = (peers, chunks, rows, width)
+    dma = pltpu.SemaphoreType.DMA
+    hbm = pl.BlockSpec(memory_space=pl.ANY)
+    vmem = pl.BlockSpec(memory_space=pltpu.VMEM)
+    out, mixed, bounded = pl.pallas_call(
+        forward_kernel,
+        out_shape=[
+            jax.ShapeDtypeStruct(blocks, BF),
+            jax.ShapeDtypeStruct((own, side, order), BF),
+            jax.ShapeDtypeStruct((own, side, order), F32),
+        ],
+        in_specs=[hbm, vmem, vmem, vmem],
+        out_specs=[hbm, vmem, vmem],
+        scratch_shapes=[
+            pltpu.VMEM(blocks, BF), pltpu.VMEM(blocks, BF),
+            pltpu.VMEM((side, rows, order), F32), pltpu.VMEM((side, rows, order), F32),
+            dma((chunks, peers)), dma((chunks, peers)), dma((chunks, peers)), dma((chunks, peers)),
+            dma((chunks,)), dma((chunks,)),
+        ],
+        compiler_params=pltpu.CompilerParams(
+            collective_id=0, has_side_effects=True, vmem_limit_bytes=32 * 1024 * 1024
+        ),
+    )(act.reshape(blocks), left, right, clip)
+    return out.reshape(tok_rows, width), mixed, bounded
 
 
 def backward_kernel(
@@ -159,11 +264,9 @@
     flat = (peers, own, width)
     cube = (own, width_right, width_left)
     by_row = (width_right, own, width_left)
-    clipped, mixed, bounded = owner_call(
-        forward_kernel, [(flat, BF), (cube, BF), (cube, F32)], by_row,
-        exchange(activations), left_factor, right_factor, clip_scale,
-    )
-    clipped = exchange(clipped).reshape(tok_rows, width)
+    clipped, mixed, bounded = forward(
+        activations, left_factor, right_factor, clip_scale, min(own, 8)
+    )
     partial_out = jnp.dot(clipped, weight_rows, preferred_element_type=F32).astype(BF)
     chips = peers // 2
     core = lax.axis_index("tensor") % 2

time: 280 us -> 250 us (0.89)
  waiting for transfers between devices: 90 us -> 44.5 us
  Pallas kernels: 46.4 us -> 66.1 us
  starting transfers between devices: 16.4 us -> 8.22 us
  local copies, waits for them, and re-layouts: 6.86 us -> 11.1 us
    all_to_all x3 -> x1, waiting for transfers between devices: 66.6 us -> 21.3 us  [exchange(): lax.all_to_all(blocks.reshape(tok_rows, width), 'tensor', split_axis=0, c...]
    pallas_call x0 -> x1, Pallas kernels: none -> 45 us  [forward(): pl.pallas_call(forward_kernel, out_shape=[jax.ShapeDtypeStruct(blocks, BF...]
    pallas_call x2 -> x1, Pallas kernels: 37.5 us -> 12.3 us  [owner_call(): pl.pallas_call(kernel, out_shape=[jax.ShapeDtypeStruct(*out) for out in o...]
    all_to_all x3 -> x1, starting transfers between devices: 12.8 us -> 3.9 us  [exchange(): lax.all_to_all(blocks.reshape(tok_rows, width), 'tensor', split_axis=0, c...]
    unnamed x13 -> x17, local copies, waits for them, and re-layouts: 4.15 us -> 8.4 us
  transfers between devices with their start and end apart: 6 -> 4, of which waited for: 6 -> 4; matrix products, arithmetic and copies ran while one was open for 1% -> 1% of each run, Pallas kernels for 0% -> 0%
where the time goes in v1:
time: 250 us
  blocking collectives  80.2 us (32%)
  Pallas kernels  66.1 us (26%)
  waiting for transfers between devices  44.5 us (18%)
  matrix products  32.7 us (13%)
  local copies, waits for them, and re-layouts  11.1 us (4%)
  starting transfers between devices  8.22 us (3%)
  other arithmetic  6.02 us (2%)
    pallas_call x1, Pallas kernels, forward(): pl.pallas_call(forward_kernel, out_shape=[jax.ShapeDtypeStruct(blocks, BF...  45 us
    all_to_all x1, blocking collectives, exchange(): lax.all_to_all(blocks.reshape(tok_rows, width), 'tensor', split_axis=0, c...  27.4 us
    all_to_all x2, blocking collectives, spread(): return lax.all_to_all(copies, axis, split_axis=0, concat_axis=0, tiled=True)  22.8 us
    all_to_all x1, waiting for transfers between devices, exchange(): lax.all_to_all(blocks.reshape(tok_rows, width), 'tensor', split_axis=0, c...  21.3 us
    all_to_all x1, blocking collectives, local(): lax.all_to_all(jnp.broadcast_to(mine[None], (chips, *mine.shape)), 'tenso...  19.3 us
    all_to_all x1, waiting for transfers between devices, local(): lax.all_to_all(paired, 'tensor', split_axis=0, concat_axis=0, axis_index_...  17.2 us
    dot_general x1, matrix products, local(): lax.dot_general(out_grad, weight_rows, (((1,), (1,)), ((), ())), preferre...  16.4 us
    dot_general x1, matrix products, local(): jnp.dot(clipped, weight_rows, preferred_element_type=F32).astype(BF)  16.3 us
  transfers between devices with their start and end apart: 4, of which 4 were waited for; matrix products, arithmetic and copies ran while one was open for 1% of the time, Pallas kernels for 0%

profile of v1, /device:TPU:0, one launch (start us, length us, event | category | flops | bytes accessed | tf_op | source)
XLA Modules:
  0.0 249.7 jit_solution(15187813481390703146)
XLA Ops:
  0.6 1.0 copy.12.clip_ref
  1.7 0.0 copy-start
  1.7 1.5 copy-done
  3.1 0.0 copy-start.4
  3.1 0.9 copy-done.4
  4.1 0.0 copy-start.6
  4.1 0.8 copy-done.6
  4.9 45.0 %shard_map.85 = (bf16[8,4,8,3456]{3,2,1,0:T(8,128)(2,1)S(1)}, bf16[32,128,216]{2,1,0:T(8,128)(2,1)S(1)}, f32[32,128,216]{2,1,0:T(8,128)S(1)}) custom-call(bf16[8,4,8,3456]{3,2,1,0:T(8,128)(2,1)S(1)} %bitcast.24, f32[216,216]{1,0:T(8,128)S(1)} %copy-done.4, f32[128,128]{1,0:T(8,128)S(1)} %copy-done.6, f32[128,216]{1,0:T(8,128)S(1)} %copy.12.clip_ref), custom_call_target="tpu_custom_call" | custom-call | tf_op jit(solution)/shard_map/pallas_call | solution.py:189
  49.9 0.0 copy-start.2
  49.9 1.9 copy-done.2
  51.9 0.0 copy-start.3
  51.9 1.3 copy-done.3
  53.2 16.3 %convolution_convert_fusion = bf16[256,5120]{1,0:T(8,128)(2,1)S(1)} fusion(bf16[256,3456]{1,0:T(8,128)(2,1)S(1)} %bitcast.25, bf16[3456,5120]{1,0:T(8,128)(2,1)} %param.10), kind=kOutput, calls=%fused_computation | convolution fusion | flops 9061007360 | bytes 39780352 | tf_op jit(solution)/shard_map/dot_general | solution.py:270
  69.5 1.2 dynamic-slice_bitcast_fusion
  70.7 0.8 collective-permute-start
  71.5 3.0 %collective-permute-done = bf16[4,32,5120]{2,1,0:T(8,128)(2,1)} collective-permute-done((bf16[4,32,5120]{2,1,0:T(8,128)(2,1)}, bf16[4,32,5120]{2,1,0:T(8,128)(2,1)}, u32[]{:S(2)}, u32[]{:S(2)}) %collective-permute-start) | collective-permute-done | bytes 1310752 | tf_op jit(solution)/shard_map/ppermute | solution.py:278
  74.5 2.7 %fusion = bf16[4,32,5120]{2,1,0:T(8,128)(2,1)} fusion(bf16[4,32,5120]{2,1,0:T(8,128)(2,1)} %collective-permute-done, bf16[4,2,32,5120]{3,2,1,0:T(8,128)(2,1)S(1)} %bitcast.27, s32[]{:T(128)S(6)} %select_n.31), kind=kLoop, calls=%fused_computation.4 | loop fusion | flops 2621440 | bytes 3932164 | tf_op jit(solution)/shard_map/convert_element_type | solution.py:279
  77.2 3.5 %all-to-all-start = ((bf16[4,32,5120]{2,1,0:T(8,128)(2,1)}), bf16[4,32,5120]{2,1,0:T(8,128)(2,1)S(1)}, u32[]{:S(2)}, u32[]{:S(2)}) async-start(bf16[4,32,5120]{2,1,0:T(8,128)(2,1)} %fusion), calls=%async_computation | async-start | bytes 2621440 | tf_op jit(solution)/shard_map/all_to_all | solution.py:280
  80.7 17.2 %all-to-all-done = bf16[4,32,5120]{2,1,0:T(8,128)(2,1)S(1)} async-done(((bf16[4,32,5120]{2,1,0:T(8,128)(2,1)}), bf16[4,32,5120]{2,1,0:T(8,128)(2,1)S(1)}, u32[]{:S(2)}, u32[]{:S(2)}) %all-to-all-start) | async-done | bytes 1310752 | tf_op jit(solution)/shard_map/all_to_all | solution.py:280
  98.0 0.2 convert_reduce_fusion
  98.1 1.1 subtract_convert_fusion
  99.2 0.1 broadcast_in_dim.6
  99.3 19.3 %all_to_all.42 = bf16[4,32,5120]{2,1,0:T(8,128)(2,1)S(1)} all-to-all(bf16[4,32,5120]{2,1,0:T(8,128)(2,1)S(1)} %broadcast_in_dim.6), channel_id=1, replica_groups={{0,2,4,6},{1,3,5,7},{8,10,12,14},{9,11,13,15},{16,18,20,22},{17,19,21,2..., dimensions={0} | all-to-all | bytes 2621440 | tf_op jit(solution)/shard_map/all_to_all | solution.py:286
  118.7 0.0 collective-permute-start.1
  118.7 3.0 %collective-permute-done.1 = bf16[4,32,5120]{2,1,0:T(8,128)(2,1)S(1)} collective-permute-done((bf16[4,32,5120]{2,1,0:T(8,128)(2,1)S(1)}, bf16[4,32,5120]{2,1,0:T(8,128)(2,1)S(1)}, u32[]{:S(2)}, u32[]{:S(2)}) %collective-permute-start.1) | collective-permute-done | bytes 1310752 | tf_op jit(solution)/shard_map/ppermute | solution.py:290
  121.7 0.2 select_bitcast_fusion.1
  121.9 0.2 pad_maximum_fusion
  122.1 16.4 %convolution_convert_fusion.1 = bf16[256,3456]{1,0:T(8,128)(2,1)} fusion(bf16[256,5120]{1,0:T(8,128)(2,1)S(1)} %bitcast.28, bf16[3456,5120]{1,0:T(8,128)(2,1)} %param.10), kind=kOutput, calls=%fused_computation.1 | convolution fusion | flops 9060581376 | bytes 39780352 | tf_op jit(solution)/shard_map/dot_general | solution.py:294
  138.5 27.4 %all_to_all.43.grad_ref = bf16[8,32,3456]{2,1,0:T(8,128)(2,1)} all-to-all(bf16[8,32,3456]{2,1,0:T(8,128)(2,1)} %bitcast.29), channel_id=1, replica_groups=mesh['dp'=4,'tensor'=8] {'tensor'}, dimensions={0} | all-to-all | bytes 3538944 | tf_op jit(solution)/shard_map/all_to_all | solution.py:259
  165.9 12.3 %shard_map.86 = (bf16[8,32,3456]{2,1,0:T(8,128)(2,1)}, f32[128,128]{1,0:T(8,128)}) custom-call(bf16[8,32,3456]{2,1,0:T(8,128)(2,1)} %all_to_all.43.grad_ref, bf16[32,128,216]{2,1,0:T(8,128)(2,1)} %copy-done.3, f32[32,128,216]{2,1,0:T(8,128)} %copy-done.2, f32[128,128]{1,0:T(8,128)} %right_ref.3), custom_call_target="tpu_custom_call" | custom-call | tf_op jit(solution)/shard_map/pallas_call | solution.py:240
  178.2 0.0 copy-start.1
  178.2 3.9 %all-to-all-start.3 = ((bf16[8,32,3456]{2,1,0:T(8,128)(2,1)}), bf16[8,32,3456]{2,1,0:T(8,128)(2,1)S(1)}, u32[]{:S(2)}, u32[]{:S(2)}) async-start(bf16[8,32,3456]{2,1,0:T(8,128)(2,1)} %get-tuple-element.13), calls=%async_computation.3 | async-start | bytes 3538944 | tf_op jit(solution)/shard_map/all_to_all | solution.py:259
  182.1 1.6 convert_element_type.43.factor_ref
  183.7 21.3 %all-to-all-done.3 = bf16[8,32,3456]{2,1,0:T(8,128)(2,1)S(1)} async-done(((bf16[8,32,3456]{2,1,0:T(8,128)(2,1)}), bf16[8,32,3456]{2,1,0:T(8,128)(2,1)S(1)}, u32[]{:S(2)}, u32[]{:S(2)}) %all-to-all-start.3) | async-done | bytes 1769504 | tf_op jit(solution)/shard_map/all_to_all | solution.py:259
  204.9 0.0 copy-done.1
  204.9 0.0 copy-start.5
  204.9 0.9 copy-done.5
  205.8 0.0 copy-start.7
  205.8 8.9 %shard_map.87 = (f32[256,3456]{1,0:T(8,128)}, f32[216,216]{1,0:T(8,128)S(1)}) custom-call(bf16[256,3456]{1,0:T(8,128)(2,1)S(1)} %bitcast.23, bf16[256,3456]{1,0:T(8,128)(2,1)S(1)} %copy-done.1, bf16[216,216]{1,0:T(8,128)(2,1)S(1)} %copy-done.5), custom_call_target="tpu_custom_call" | custom-call | flops 764411904 | bytes 7077888 | tf_op jit(solution)/shard_map/pallas_call | solution.py:37
  214.7 0.0 copy-done.7
  214.8 10.7 %all_to_all.44 = f32[8,48,216]{2,1,0:T(8,128)S(1)} all-to-all(f32[8,48,216]{2,1,0:T(8,128)S(1)} %bitcast.30), channel_id=1, replica_groups=mesh['dp'=4,'tensor'=8] {'tensor'}, dimensions={0} | all-to-all | bytes 663552 | tf_op jit(solution)/shard_map/all_to_all | solution.py:319
  225.5 12.0 %all_to_all.45 = f32[4,48,216]{2,1,0:T(8,128)S(1)} all-to-all(f32[4,48,216]{2,1,0:T(8,128)S(1)} %broadcast_in_dim.7), channel_id=1, replica_groups=mesh['dp'=4,'tensor'=8] {'dp'}, dimensions={0} | all-to-all | bytes 331776 | tf_op jit(solution)/shard_map/all_to_all | solution.py:317
  237.6 10.7 %all_to_all.46 = f32[8,48,216]{2,1,0:T(8,128)S(1)} all-to-all(f32[8,48,216]{2,1,0:T(8,128)S(1)} %broadcast_in_dim.8), channel_id=1, replica_groups=mesh['dp'=4,'tensor'=8] {'tensor'}, dimensions={0} | all-to-all | bytes 663552 | tf_op jit(solution)/shard_map/all_to_all | solution.py:317
  248.3 0.7 slice.8
  249.0 0.6 slice.9
  (6 shorter events, 0.1 us)
Async XLA Ops:
  1.7 1.5 copy-start
  3.1 0.9 copy-start.4
  4.1 0.8 copy-start.6
  49.9 1.9 copy-start.2
  51.9 1.3 copy-start.3
  70.7 3.8 %collective-permute-start = (bf16[4,32,5120]{2,1,0:T(8,128)(2,1)}, bf16[4,32,5120]{2,1,0:T(8,128)(2,1)}, u32[]{:S(2)}, u32[]{:S(2)}) collective-permute-start(bf16[4,32,5120]{2,1,0:T(8,128)(2,1)} %dynamic-slice_bitcast_fusion), channel_id=1, source_target_pairs={{0,1},{1,0},{2,3},{3,2},{4,5},{5,4},{6,7},{7,6},{8,9},{9,8},{10,11... | collective-permute-start | bytes 3932168 | tf_op jit(solution)/shard_map/ppermute | solution.py:278
  77.2 20.8 %all-to-all-start = ((bf16[4,32,5120]{2,1,0:T(8,128)(2,1)}), bf16[4,32,5120]{2,1,0:T(8,128)(2,1)S(1)}, u32[]{:S(2)}, u32[]{:S(2)}) async-start(bf16[4,32,5120]{2,1,0:T(8,128)(2,1)} %fusion), calls=%async_computation | async-start | bytes 2621440 | tf_op jit(solution)/shard_map/all_to_all | solution.py:280
  118.7 3.0 %collective-permute-start.1 = (bf16[4,32,5120]{2,1,0:T(8,128)(2,1)S(1)}, bf16[4,32,5120]{2,1,0:T(8,128)(2,1)S(1)}, u32[]{:S(2)}, u32[]{:S(2)}) collective-permute-start(bf16[4,32,5120]{2,1,0:T(8,128)(2,1)S(1)} %all_to_all.42), channel_id=1, source_target_pairs={{0,1},{1,0},{2,3},{3,2},{4,5},{5,4},{6,7},{7,6},{8,9},{9,8},{10,11... | collective-permute-start | bytes 3932168 | tf_op jit(solution)/shard_map/ppermute | solution.py:290
  178.2 26.8 %copy-start.1 = (bf16[256,3456]{1,0:T(8,128)(2,1)S(1)}, bf16[256,3456]{1,0:T(8,128)(2,1)}, u32[]{:S(2)}) copy-start(bf16[256,3456]{1,0:T(8,128)(2,1)} %act_ref.1) | copy-start | bytes 5308420
  178.2 26.8 %all-to-all-start.3 = ((bf16[8,32,3456]{2,1,0:T(8,128)(2,1)}), bf16[8,32,3456]{2,1,0:T(8,128)(2,1)S(1)}, u32[]{:S(2)}, u32[]{:S(2)}) async-start(bf16[8,32,3456]{2,1,0:T(8,128)(2,1)} %get-tuple-element.13), calls=%async_computation.3 | async-start | bytes 3538944 | tf_op jit(solution)/shard_map/all_to_all | solution.py:259
  204.9 0.9 copy-start.5
  205.8 8.9 %copy-start.7 = (f32[128,128]{1,0:T(8,128)S(1)}, f32[128,128]{1,0:T(8,128)}, u32[]{:S(2)}) copy-start(f32[128,128]{1,0:T(8,128)} %get-tuple-element.15) | copy-start | bytes 196612

commit v2 on v0

v2 whole, which is shorter than its diff:
```python
import jax
import jax.numpy as jnp
from jax import lax
from jax.experimental import pallas as pl
from jax.experimental.pallas import tpu as pltpu
from jax.sharding import PartitionSpec as P

BF = jnp.bfloat16
F32 = jnp.float32
MESH = pl.DeviceIdType.MESH


def split(value):
    head = value.astype(BF)
    return head, (value - head.astype(F32)).astype(BF)


def dot(a, b, dims):
    return lax.dot_general(a, b, ((dims[:1], dims[1:]), ((), ())), preferred_element_type=F32)


def to_peer(src, dst, send, recv, peer):
    return pltpu.make_async_remote_copy(
        src_ref=src, dst_ref=dst, send_sem=send, recv_sem=recv,
        device_id={"tensor": peer}, device_id_type=MESH,
    )


def to_layer(src, dst, send, recv, layer):
    return pltpu.make_async_remote_copy(
        src_ref=src, dst_ref=dst, send_sem=send, recv_sem=recv,
        device_id={"dp": layer}, device_id_type=MESH,
    )


def others(me, count, body):
    @pl.loop(1, count)
    def _(o):
        body(lax.rem(me + o, count))


def kernel(
    act_ref, left_ref, right_ref, clip_ref, weight_ref, target_ref,
    out_ref, sums_ref,
    x_ref, send_ref, recv_ref,
    mixed_ref, slope_ref, rows_ref, cols_ref,
    w_ref, lhs_ref, aim_ref, part_ref, pair_ref, paired_ref, got_ref, grad_ref, acc_ref,
    left_acc, right_acc, stack_ref, shares_ref, layers_ref, total_ref,
    in_send, in_recv, fwd_send, fwd_recv, bwd_send, bwd_recv, end_send, end_recv,
    own_in, own_fwd, own_bwd, own_end, w_sem, aim_sem,
    pair_send, pair_recv, chip_send, chip_recv, all_send, all_recv, relay_send,
    share_send, share_recv, layer_send, layer_recv, sum_send, sum_recv, own_sum,
):
    peers, chunks, rows, width = act_ref.shape
    own = chunks * rows
    order, side = left_ref.shape[0], right_ref.shape[0]
    each = width // order
    blocks, cols = w_ref.shape[0], w_ref.shape[2]
    chips = peers // 2
    layers = layers_ref.shape[0]
    me, layer = lax.axis_index("tensor"), lax.axis_index("dp")
    chip, core = me // 2, lax.rem(me, 2)
    partner = me + 1 - 2 * core

    def act_in(c, p):
        return to_peer(act_ref.at[p, c], x_ref.at[me, c], in_send.at[c, p], in_recv.at[c, me], p)

    def act_got(c, s):
        return to_peer(act_ref.at[s, c], x_ref.at[s, c], in_send.at[c, s], in_recv.at[c, s], s)

    def act_own(c):
        return pltpu.make_async_copy(act_ref.at[me, c], x_ref.at[me, c], own_in.at[c])

    def fwd_out(c, p):
        return to_peer(send_ref.at[p, c], recv_ref.at[me, c], fwd_send.at[c, p], fwd_recv.at[c, me], p)

    def fwd_got(c, s):
        return to_peer(send_ref.at[s, c], recv_ref.at[s, c], fwd_send.at[c, s], fwd_recv.at[c, s], s)

    def fwd_own(c):
        return pltpu.make_async_copy(send_ref.at[me, c], recv_ref.at[me, c], own_fwd.at[c])

    def bwd_out(c, p):
        return to_peer(send_ref.at[p, c], recv_ref.at[me, c], bwd_send.at[c, p], bwd_recv.at[c, me], p)

    def bwd_got(c, s):
        return to_peer(send_ref.at[s, c], recv_ref.at[s, c], bwd_send.at[c, s], bwd_recv.at[c, s], s)

    def bwd_own(c):
        return pltpu.make_async_copy(send_ref.at[me, c], recv_ref.at[me, c], own_bwd.at[c])

    def end_out(c, p):
        return to_peer(send_ref.at[p, c], out_ref.at[me, c], end_send.at[c, p], end_recv.at[c, me], p)

    def end_got(c, s):
        return to_peer(send_ref.at[s, c], out_ref.at[s, c], end_send.at[c, s], end_recv.at[c, s], s)

    def end_own(c):
        return pltpu.make_async_copy(send_ref.at[me, c], out_ref.at[me, c], own_end.at[c])

    def load_w(n):
        here = pl.ds(pl.multiple_of(n * cols, cols), cols)
        return pltpu.make_async_copy(weight_ref.at[:, here], w_ref.at[n], w_sem.at[n])

    def load_aim(n):
        here = pl.ds(pl.multiple_of(n * cols, cols), cols)
        return pltpu.make_async_copy(target_ref.at[me, :, here], aim_ref.at[n], aim_sem.at[n])

    def pair_out(n):
        return to_peer(
            part_ref.at[n, 1 - core], pair_ref.at[n], pair_send.at[n], pair_recv.at[n], partner
        )

    def chip_out(n, q):
        return to_peer(
            paired_ref.at[n, q], got_ref.at[n, chip],
            chip_send.at[n, q], chip_recv.at[n, chip], 2 * q + core,
        )

    def chip_got(n, q):
        return to_peer(
            paired_ref.at[n, q], got_ref.at[n, q],
            chip_send.at[n, q], chip_recv.at[n, q], 2 * q + core,
        )

    def all_out(n, p):
        return to_peer(
            grad_ref.at[n, me], grad_ref.at[n, me], all_send.at[n, p], all_recv.at[n, me], p
        )

    def all_got(n, s):
        return to_peer(
            grad_ref.at[n, s], grad_ref.at[n, s], all_send.at[n, s], all_recv.at[n, s], partner
        )

    def relay(n, q):
        s = 2 * q + core
        return to_peer(
            grad_ref.at[n, s], grad_ref.at[n, s], relay_send.at[n, q], all_recv.at[n, s], partner
        )

    def share_out(p):
        return to_peer(
            stack_ref.at[p], shares_ref.at[me], share_send.at[p], share_recv.at[me], p
        )

    def share_got(s):
        return to_peer(stack_ref.at[s], shares_ref.at[s], share_send.at[s], share_recv.at[s], s)

    def layer_out(d):
        return to_layer(
            layers_ref.at[layer], layers_ref.at[layer], layer_send.at[d], layer_recv.at[layer], d
        )

    def layer_got(d):
        return to_layer(layers_ref.at[d], layers_ref.at[d], layer_send.at[d], layer_recv.at[d], d)

    def sum_out(p):
        return to_peer(total_ref, sums_ref.at[me], sum_send.at[p], sum_recv.at[me], p)

    def sum_got(s):
        return to_peer(total_ref, sums_ref.at[s], sum_send.at[s], sum_recv.at[s], s)

    barrier = pltpu.get_barrier_semaphore()
    others(me, peers, lambda p: pl.semaphore_signal(
        barrier, inc=1, device_id={"tensor": p}, device_id_type=MESH))
    others(layer, layers, lambda d: pl.semaphore_signal(
        barrier, inc=1, device_id={"dp": d}, device_id_type=MESH))
    pl.semaphore_wait(barrier, peers + layers - 2)

    @pl.loop(0, chunks)
    def _(c):
        act_own(c).start()
        others(me, peers, lambda p: act_in(c, p).start())

    @pl.loop(0, blocks)
    def _(n):
        load_w(n).start()
        load_aim(n).start()

    left_hi, left_lo = split(left_ref[...])
    right_hi, right_lo = split(right_ref[...])
    clip = clip_ref[...]

    @pl.loop(0, chunks)
    def _(c):
        act_own(c).wait()
        others(me, peers, lambda s: act_got(c, s).wait_recv())

        @pl.loop(0, peers)
        def _(s):
            x = jnp.concatenate(
                [x_ref[s, c, :, j * order : (j + 1) * order] for j in range(each)], axis=0
            )
            mixed = dot(x, left_hi, (1, 0)) + dot(x, left_lo, (1, 0))
            for j in range(each):
                rows_ref[s * each + j] = mixed[j * rows : (j + 1) * rows]

        @pl.loop(0, rows, unroll=4)
        def _(t):
            mixed = rows_ref[:, t, :]
            hi, lo = split(mixed)
            mixed_ref[c * rows + t] = hi
            rotated = (
                dot(right_hi, hi, (0, 0)) + dot(right_lo, hi, (0, 0)) + dot(right_hi, lo, (0, 0))
            )
            bounded = jnp.tanh(rotated / clip)
            slope_ref[c * rows + t] = (1.0 - bounded * bounded).astype(BF)
            cols_ref[:, t, :] = clip * bounded

        @pl.loop(0, peers)
        def _(s):
            for j in range(each):
                send_ref[s, c, :, j * order : (j + 1) * order] = cols_ref[s * each + j].astype(BF)

        fwd_own(c).start()
        others(me, peers, lambda p: fwd_out(c, p).start())

    @pl.loop(0, chunks)
    def _(c):
        fwd_own(c).wait()
        others(me, peers, lambda s: fwd_got(c, s).wait_recv())

    @pl.loop(0, peers)
    def _(s):
        lhs_ref[s] = jnp.concatenate([recv_ref[s, c] for c in range(chunks)], axis=0)

    acc_ref[...] = jnp.zeros_like(acc_ref)

    def stage(i, lag):
        return pl.when((i >= lag) & (i < blocks + lag))

    @pl.loop(0, blocks + LAGS[4])
    def _(i):
        @stage(i, LAGS[0])
        def _():
            n = i - LAGS[0]
            load_w(n).wait()
            lhs = jnp.concatenate([lhs_ref[s] for s in range(peers)], axis=0)
            full = dot(lhs, w_ref[n], (1, 0))
            for p in range(peers):
                part_ref[n, p % 2, p // 2] = full[p * own : (p + 1) * own].astype(BF)
            pair_out(n).start()

        @stage(i, LAGS[1])
        def _():
            n = i - LAGS[1]
            pair_out(n).wait_recv()
            paired_ref[n] = (part_ref[n, core].astype(F32) + pair_ref[n].astype(F32)).astype(BF)
            others(chip, chips, lambda q: chip_out(n, q).start())

        @stage(i, LAGS[2])
        def _():
            n = i - LAGS[2]
            load_aim(n).wait()
            total = paired_ref[n, chip].astype(F32)
            for o in range(1, chips):
                q = lax.rem(chip + o, chips)
                chip_got(n, q).wait_recv()
                total = total + got_ref[n, q].astype(F32)
            grad_ref[n, me] = (total - aim_ref[n].astype(F32)).astype(BF)
            all_out(n, partner).start()
            others(chip, chips, lambda q: all_out(n, 2 * q + core).start())

        @stage(i, LAGS[3])
        def _():
            n = i - LAGS[3]

            def forward(q):
                all_got(n, 2 * q + core).wait_recv()
                relay(n, q).start()

            others(chip, chips, forward)

        @stage(i, LAGS[4])
        def _():
            n = i - LAGS[4]

            @pl.loop(0, chips)
            def _(q):
                all_got(n, 2 * q + 1 - core).wait_recv()

            grad = jnp.concatenate([grad_ref[n, s] for s in range(peers)], axis=0)
            for h in range(0, width, 512):
                here = slice(h, min(h + 512, width))
                acc_ref[:, here] += dot(grad, w_ref[n, here, :], (1, 1))

    @pl.loop(0, chunks)
    def _(c):
        def drain(p):
            act_in(c, p).wait_send()
            fwd_out(c, p).wait_send()

        others(me, peers, drain)

    @pl.loop(0, chunks)
    def _(c):
        @pl.loop(0, peers)
        def _(p):
            start = pl.multiple_of(p * own + c * rows, rows)
            send_ref[p, c] = acc_ref[pl.ds(start, rows), :].astype(BF)

        bwd_own(c).start()
        others(me, peers, lambda p: bwd_out(c, p).start())

    left_acc[...] = jnp.zeros_like(left_acc)
    right_acc[...] = jnp.zeros_like(right_acc)
    stack_ref[...] = jnp.zeros_like(stack_ref)

    @pl.loop(0, chunks)
    def _(c):
        bwd_own(c).wait()
        others(me, peers, lambda s: bwd_got(c, s).wait_recv())

        @pl.loop(0, peers)
        def _(s):
            for j in range(each):
                rows_ref[s * each + j] = recv_ref[s, c, :, j * order : (j + 1) * order].astype(F32)

        @pl.loop(0, rows, unroll=4)
        def _(t):
            turned = (rows_ref[:, t, :] * slope_ref[c * rows + t].astype(F32)).astype(BF)
            right_acc[...] += dot(mixed_ref[c * rows + t], turned, (1, 1))
            cols_ref[:, t, :] = dot(right_hi, turned, (1, 0))

        def unmixed(s):
            return jnp.concatenate(
                [cols_ref[s * each + j] for j in range(each)], axis=0
            ).astype(BF)

        @pl.loop(0, peers)
        def _(s):
            x = jnp.concatenate(
                [x_ref[s, c, :, j * order : (j + 1) * order] for j in range(each)], axis=0
            )
            left_acc[...] += dot(x, unmixed(s), (0, 0))

        @pl.when(c == chunks - 1)
        def _():
            deep = stack_ref.shape[1]
            half = side // 2
            for g in range(order // 8):
                at = divmod(g * 8, deep)
                stack_ref[at[0], at[1] : at[1] + 8, :order] = left_acc[g * 8 : (g + 1) * 8]
            for g in range(half // 8):
                at = divmod(order + g * 8, deep)
                here = slice(at[1], at[1] + 8)
                stack_ref[at[0], here, :side] = right_acc[g * 8 : (g + 1) * 8]
                stack_ref[at[0], here, side : 2 * side] = right_acc[half + g * 8 : half + (g + 1) * 8]
            others(me, peers, lambda p: share_out(p).start())

        others(me, peers, lambda p: bwd_out(c, p).wait_send())

        @pl.loop(0, peers)
        def _(s):
            grad = dot(unmixed(s), left_hi, (1, 1)).astype(BF)
            for j in range(each):
                send_ref[s, c, :, j * order : (j + 1) * order] = grad[j * rows : (j + 1) * rows]

        end_own(c).start()
        others(me, peers, lambda p: end_out(c, p).start())

    total = stack_ref[me]
    for o in range(1, peers):
        s = lax.rem(me + o, peers)
        share_got(s).wait_recv()
        total = total + shares_ref[s]
    layers_ref[layer] = total
    others(layer, layers, lambda d: layer_out(d).start())
    others(layer, layers, lambda d: layer_got(d).wait_recv())
    total = layers_ref[0]
    for d in range(1, layers):
        total = total + layers_ref[d]
    total_ref[...] = total
    mine = pltpu.make_async_copy(total_ref, sums_ref.at[me], own_sum)
    mine.start()
    others(me, peers, lambda p: sum_out(p).start())

    mine.wait()
    others(layer, layers, lambda d: layer_out(d).wait_send())

    def finish(p):
        share_out(p).wait_send()
        sum_out(p).wait_send()
        sum_got(p).wait_recv()

    others(me, peers, finish)

    @pl.loop(0, chunks)
    def _(c):
        end_own(c).wait()

        def drain(p):
            end_out(c, p).wait_send()
            end_got(c, p).wait_recv()

        others(me, peers, drain)

    @pl.loop(0, blocks)
    def _(n):
        pair_out(n).wait_send()
        all_out(n, partner).wait_send()

        def drain(q):
            chip_out(n, q).wait_send()
            all_out(n, 2 * q + core).wait_send()
            relay(n, q).wait_send()

        others(chip, chips, drain)


LAGS = (0, 1, 3, 5, 6)


def local(activations, left_factor, right_factor, clip_scale, weight_rows, target):
    peers, layers = lax.axis_size("tensor"), lax.axis_size("dp")
    tokens, width = activations.shape
    order, side = left_factor.shape[0], right_factor.shape[0]
    out = weight_rows.shape[1]
    own = tokens // peers
    rows = min(own, 8)
    chunks = own // rows
    chips = peers // 2
    cols = next(b for b in (512, 256, 128) if out % b == 0)
    blocks = out // cols
    lanes = -(-max(order, 2 * side) // 128) * 128
    deep = -(-(order + side // 2) // (8 * peers)) * 8
    flat = (peers, chunks, rows, width)
    cube = (own, side, order)
    by_row = (side, rows, order)
    piece = (peers, deep, lanes)
    dma = pltpu.SemaphoreType.DMA
    hbm = pl.BlockSpec(memory_space=pl.ANY)
    vmem = pl.BlockSpec(memory_space=pltpu.VMEM)
    grid = (chunks, peers)
    scratch = (
        [pltpu.VMEM(flat, BF)] * 3
        + [pltpu.VMEM(cube, BF)] * 2
        + [pltpu.VMEM(by_row, F32)] * 2
        + [
            pltpu.VMEM((blocks, width, cols), BF),
            pltpu.VMEM((peers, own, width), BF),
            pltpu.VMEM((blocks, own, cols), BF),
            pltpu.VMEM((blocks, 2, chips, own, cols), BF),
            pltpu.VMEM((blocks, chips, own, cols), BF),
            pltpu.VMEM((blocks, chips, own, cols), BF),
            pltpu.VMEM((blocks, chips, own, cols), BF),
            pltpu.VMEM((blocks, peers, own, cols), BF),
            pltpu.VMEM((tokens, width), F32),
            pltpu.VMEM((order, order), F32),
            pltpu.VMEM((side, side), F32),
            pltpu.VMEM(piece, F32),
            pltpu.VMEM(piece, F32),
            pltpu.VMEM((layers, deep, lanes), F32),
            pltpu.VMEM((deep, lanes), F32),
        ]
        + [dma(grid)] * 8
        + [dma((chunks,))] * 4
        + [dma((blocks,))] * 4
        + [dma((blocks, chips))] * 2
        + [dma((blocks, peers))] * 2
        + [dma((blocks, chips))]
        + [dma((peers,))] * 2
        + [dma((layers,))] * 2
        + [dma((peers,))] * 2
        + [dma]
    )
    grad, sums = pl.pallas_call(
        kernel,
        out_shape=[jax.ShapeDtypeStruct(flat, BF), jax.ShapeDtypeStruct(piece, F32)],
        in_specs=[hbm, vmem, vmem, vmem, hbm, hbm],
        out_specs=[hbm, hbm],
        scratch_shapes=scratch,
        compiler_params=pltpu.CompilerParams(
            collective_id=0, has_side_effects=True, vmem_limit_bytes=67043328
        ),
    )(
        activations.reshape(flat), left_factor, right_factor, clip_scale,
        weight_rows, target.reshape(peers, own, out),
    )
    sums = sums.reshape(peers * deep, lanes)
    low = sums[order : order + side // 2]
    right_sum = jnp.concatenate([low[:, :side], low[:, side : 2 * side]], axis=0)
    return (sums[:order, :order], right_sum, grad.reshape(tokens, width).astype(F32))


def solution(mesh):
    placed = (P("dp", "tensor"), P(), P(), P(), P("tensor", None), P("dp", None))
    return jax.shard_map(
        local, mesh=mesh, in_specs=placed, out_specs=(P(), P(), P("dp", "tensor")), check_vma=False
    )
```

time: 280 us -> 149 us (0.53)
  Pallas kernels: 46.4 us -> 140 us
  waiting for transfers between devices: 90 us -> 0 us
  blocking collectives: 79.9 us -> 0 us
  matrix products: 32.9 us -> 0 us
  starting transfers between devices: 16.4 us -> 0 us
    pallas_call x3 -> x1, Pallas kernels: 46.4 us -> 140 us  [local(): pl.pallas_call(kernel, out_shape=[jax.ShapeDtypeStruct(flat, BF), jax.Sha...]
    all_to_all x4 -> x0, waiting for transfers between devices: 83.6 us -> none  [the longest x3 66.6 us: exchange(): lax.all_to_all(blocks.reshape(tok_rows, width), 'tensor', split_axis=0, c...]
    all_to_all x5 -> x0, blocking collectives: 79.9 us -> none  [the longest x1 27.4 us: exchange(): lax.all_to_all(blocks.reshape(tok_rows, width), 'tensor', split_axis=0, c...]
    dot_general x2 -> x0, matrix products: 32.9 us -> none  [the longest x1 16.5 us: local(): jnp.dot(clipped, weight_rows, preferred_element_type=F32).astype(BF)]
    all_to_all x4 -> x0, starting transfers between devices: 16.4 us -> none  [the longest x3 12.8 us: exchange(): lax.all_to_all(blocks.reshape(tok_rows, width), 'tensor', split_axis=0, c...]
    ppermute x2 -> x0, waiting for transfers between devices: 6.41 us -> none  [the longest x1 3.37 us: local(): there = lax.ppermute(there, 'tensor', swap)]
  transfers between devices with their start and end apart: 6 -> 0, of which waited for: 6 -> 0; matrix products, arithmetic and copies ran while one was open for 1% -> 0% of each run, Pallas kernels for 0% -> 0%
where the time goes in v2:
time: 149 us
  Pallas kernels  140 us (94%)
  other arithmetic  4.13 us (3%)
  local copies, waits for them, and re-layouts  4.07 us (3%)
    pallas_call x1, Pallas kernels, local(): pl.pallas_call(kernel, out_shape=[jax.ShapeDtypeStruct(flat, BF), jax.Sha...  140 us
    convert_element_type x1, other arithmetic, local(): grad.reshape(tokens, width).astype(F32)  3.5 us

profile of v2, /device:TPU:0, one launch (start us, length us, event | category | flops | bytes accessed | tf_op | source)
XLA Modules:
  0.0 148.6 jit_solution(17278144415573056919)
XLA Ops:
  0.6 1.7 %copy.9.clip_ref = f32[128,216]{1,0:T(8,128)} copy(f32[128,216]{0,1:T(8,128)} %param.9) | data formatting | bytes 221184 | tf_op args[3]
  2.3 139.7 %shard_map.85 = (bf16[8,4,8,3456]{3,2,1,0:T(8,128)(2,1)}, f32[8,40,256]{2,1,0:T(8,128)}) custom-call(bf16[8,4,8,3456]{3,2,1,0:T(8,128)(2,1)} %bitcast.7, f32[216,216]{1,0:T(8,128)} %left_ref.1, f32[128,128]{1,0:T(8,128)} %right_ref.1, f32[128,216]{1,0:T(8,128)} %copy.9.clip_ref, bf16[3456,5120]{1,0:T(8,128)(2,1)} %weight_ref.1, bf16[8,32,5120]{2,1,0:T(8,128)(2,1)} %bitcast.6), custom_call_target="tpu_custom_call" | custom-call | tf_op jit(solution)/shard_map/pallas_call | solution.py:468
  142.0 0.8 fusion
  142.8 1.6 %slice.15 = f32[216,216]{1,0:T(8,128)} slice(f32[320,256]{1,0:T(8,128)} %bitcast.9), slice={[0:216], [0:216]} | slice | bytes 373248 | tf_op jit(solution)/shard_map/slice | solution.py:484
  144.4 0.6 pad_maximum_fusion
  145.1 3.5 %bitcast_convert_fusion = f32[256,3456]{1,0:T(8,128)} fusion(bf16[8,4,8,3456]{3,2,1,0:T(8,128)(2,1)} %get-tuple-element.6), kind=kLoop, calls=%fused_computation | loop fusion | flops 884736 | bytes 5308416 | tf_op jit(solution)/shard_map/convert_element_type | solution.py:484

commit v3 on v0

v3 whole, which is shorter than its diff:
```python
import jax
import jax.numpy as jnp
from jax import lax
from jax.experimental import pallas as pl
from jax.experimental.pallas import tpu as pltpu
from jax.sharding import PartitionSpec as P

BF = jnp.bfloat16
F32 = jnp.float32
MESH = pl.DeviceIdType.MESH
LAGS = (0, 1, 3, 5, 7, 9, 10)


def split(value):
    head = value.astype(BF)
    return head, (value - head.astype(F32)).astype(BF)


def dot(a, b, dims):
    return lax.dot_general(a, b, ((dims[:1], dims[1:]), ((), ())), preferred_element_type=F32)


def remote(src, dst, send, recv, **where):
    return pltpu.make_async_remote_copy(
        src_ref=src, dst_ref=dst, send_sem=send, recv_sem=recv,
        device_id=where, device_id_type=MESH,
    )


def wait_for(ref, sem):
    pltpu.make_async_copy(ref, ref, sem).wait()


def others(me, count, body):
    @pl.loop(1, count)
    def _(o):
        body(lax.rem(me + o, count))


def kernel(
    act_ref, left_ref, right_ref, clip_ref, weight_ref, target_ref,
    out_ref, sums_ref,
    x_ref, send_ref, recv_ref,
    tall_ref, mixed_ref, slope_ref, rows_ref, cube_ref,
    w_ref, lhs_ref, aim_ref, part_ref, pair_ref, got_ref, last_ref, grad_ref, acc_ref,
    left_acc, right_acc, stack_ref, terms_ref, shares_ref, layers_ref, total_ref,
    in_send, in_recv, fwd_send, fwd_recv, bwd_send, bwd_recv, end_send, end_recv,
    w_sem, aim_sem, pair_send, pair_recv, got_send, got_recv, last_send, last_recv,
    all_send, near_recv, relay_send, far_recv, twins_send, twins_recv,
    share_send, share_recv, layer_send, layer_recv, sum_send, sum_recv,
):
    peers, chunks, rows, width = act_ref.shape
    own = chunks * rows
    order, side = left_ref.shape[0], right_ref.shape[0]
    each = width // order
    blocks, cols = w_ref.shape[0], w_ref.shape[2]
    chips = peers // 2
    layers = layers_ref.shape[0]
    parts, tokens = acc_ref.shape[:2]
    share = tokens // peers
    batch = chunks // parts
    steps = parts * blocks
    wide, high = got_ref.shape[1] + 1, got_ref.shape[2]
    across = wide
    me, layer = lax.axis_index("tensor"), lax.axis_index("dp")
    chip, core = me // 2, lax.rem(me, 2)
    partner = me + 1 - 2 * core
    most = pl.ds(0, peers - 1)

    def unpack(ref, s, c):
        flat = ref[s, c].astype(F32)
        return jnp.concatenate(
            [flat[:, j * order : (j + 1) * order] for j in range(each)], axis=0
        )

    def pack(ref, s, c, value):
        flat = jnp.concatenate(
            [value[j * rows : (j + 1) * rows] for j in range(each)], axis=1
        )
        ref[s, c] = flat.astype(BF)

    def spread(src, dst, send, recv, c):
        pltpu.make_async_copy(src.at[me, c], dst.at[me, c], recv).start()
        others(me, peers, lambda p: remote(
            src.at[p, c], dst.at[me, c], send, recv, tensor=p).start())

    def load_w(n):
        here = pl.ds(pl.multiple_of(n * cols, cols), cols)
        return pltpu.make_async_copy(weight_ref.at[:, here], w_ref.at[n], w_sem.at[n])

    load_aim = pltpu.make_async_copy(target_ref.at[me], aim_ref, aim_sem)

    barrier = pltpu.get_barrier_semaphore()
    others(me, peers, lambda p: pl.semaphore_signal(
        barrier, inc=1, device_id={"tensor": p}, device_id_type=MESH))
    others(layer, layers, lambda d: pl.semaphore_signal(
        barrier, inc=1, device_id={"dp": d}, device_id_type=MESH))
    pl.semaphore_wait(barrier, peers + layers - 2)

    @pl.loop(0, chunks)
    def _(c):
        spread(act_ref, x_ref, in_send, in_recv.at[c], c)

    load_aim.start()

    @pl.loop(0, blocks)
    def _(n):
        load_w(n).start()

    left_hi, left_lo = split(left_ref[...])
    turned_hi, turned_lo = split(jnp.transpose(right_ref[...]))
    turned_wide = jnp.concatenate([turned_hi, turned_hi, turned_lo], axis=1)
    right_hi = right_ref[...].astype(BF)
    clip = jnp.transpose(clip_ref[...])
    unclip = 1.0 / clip

    def forward():
        @pl.loop(0, chunks)
        def _(c):
            wait_for(x_ref.at[:, c], in_recv.at[c])

            @pl.loop(0, peers)
            def _(s):
                x = unpack(x_ref, s, c).astype(BF)
                here = pl.ds(pl.multiple_of(s * each * rows, each * rows), each * rows)
                tall_ref[c, here] = x
                mixed = dot(x, left_hi, (1, 0)) + dot(x, left_lo, (1, 0))
                for j in range(each):
                    rows_ref[s * each + j] = mixed[j * rows : (j + 1) * rows]

            @pl.loop(0, rows, unroll=4)
            def _(t):
                mixed = rows_ref[:, t, :]
                hi, lo = split(mixed)
                mixed_ref[c * rows + t] = hi
                rotated = dot(turned_wide, jnp.concatenate([hi, lo, hi], axis=0), (1, 0))
                bounded = jnp.tanh(rotated * unclip)
                slope_ref[c * rows + t] = (1.0 - bounded * bounded).astype(BF)
                cube_ref[:, t, :] = clip * bounded

            @pl.loop(0, peers)
            def _(s):
                here = pl.ds(pl.multiple_of(s * each, each), each)
                pack(send_ref, s, c, cube_ref[here].reshape(each * rows, order))

            spread(send_ref, recv_ref, fwd_send, fwd_recv.at[c], c)

    def project():
        acc_ref[...] = jnp.zeros_like(acc_ref)
        load_aim.wait()

        def places(n):
            row, col = chip // across, lax.rem(chip, across)
            if across * across != chips:
                return col, row, lambda near, far: far * across + near
            turn = lax.rem(n, 2)

            def at(near, far):
                return (1 - turn) * (far * across + near) + turn * (near * across + far)

            return (1 - turn) * col + turn * row, (1 - turn) * row + turn * col, at

        def stage(i, lag):
            return pl.when((i >= lag) & (i < steps + lag))

        @pl.loop(0, steps + LAGS[6])
        def _(i):
            @stage(i, LAGS[0])
            def _():
                n = i - LAGS[0]
                part, block = n // blocks, lax.rem(n, blocks)

                @pl.when(block == 0)
                def _():
                    for k in range(batch):
                        c = part * batch + k
                        wait_for(recv_ref.at[:, c], fwd_recv.at[c])

                    @pl.loop(0, peers)
                    def _(s):
                        lhs_ref[s] = jnp.concatenate(
                            [recv_ref[s, part * batch + k] for k in range(batch)], axis=0
                        )

                @pl.when(part == 0)
                def _():
                    load_w(block).wait()

                lhs = jnp.concatenate([lhs_ref[s] for s in range(peers)], axis=0)
                full = dot(lhs, w_ref[block], (1, 0))
                for p in range(peers):
                    part_ref[n, p % 2, p // 2] = full[p * share : (p + 1) * share].astype(BF)
                remote(
                    part_ref.at[n, 1 - core], pair_ref.at[n], pair_send, pair_recv.at[n],
                    tensor=partner,
                ).start()

            @stage(i, LAGS[1])
            def _():
                n = i - LAGS[1]
                wait_for(pair_ref.at[n], pair_recv.at[n])
                part_ref[n, core] = (
                    part_ref[n, core].astype(F32) + pair_ref[n].astype(F32)
                ).astype(BF)
                near, far, at = places(n)
                for o in range(1, wide):
                    there = lax.rem(near + o, wide)
                    for k in range(high):
                        remote(
                            part_ref.at[n, core, at(there, k)], got_ref.at[n, o - 1, k],
                            got_send, got_recv.at[n], tensor=2 * at(there, far) + core,
                        ).start()

            @stage(i, LAGS[2])
            def _():
                n = i - LAGS[2]
                near, far, at = places(n)
                wait_for(got_ref.at[n], got_recv.at[n])
                for o in range(1, high):
                    there = lax.rem(far + o, high)
                    block = part_ref.at[n, core, at(near, there)]
                    total = block[...].astype(F32)
                    for k in range(wide - 1):
                        total = total + got_ref[n, k, there].astype(F32)
                    block[...] = total.astype(BF)
                    remote(
                        block, last_ref.at[n, o - 1], last_send, last_recv.at[n],
                        tensor=2 * at(near, there) + core,
                    ).start()

            @stage(i, LAGS[3])
            def _():
                n = i - LAGS[3]
                near, far, at = places(n)
                wait_for(last_ref.at[n], last_recv.at[n])
                total = part_ref[n, core, chip].astype(F32)
                for k in range(wide - 1):
                    total = total + got_ref[n, k, far].astype(F32)
                for k in range(high - 1):
                    total = total + last_ref[n, k].astype(F32)
                part, block = n // blocks, lax.rem(n, blocks)
                here = pl.ds(pl.multiple_of(block * cols, cols), cols)
                aim = aim_ref[pl.ds(pl.multiple_of(part * share, share), share), here]
                grad_ref[n, me] = (total - aim.astype(F32)).astype(BF)
                mine = grad_ref.at[n, me]
                for o in range(1, wide):
                    remote(
                        mine, mine, all_send, near_recv.at[n],
                        tensor=2 * at(lax.rem(near + o, wide), far) + core,
                    ).start()
                for o in range(1, high):
                    remote(
                        mine, mine, all_send, far_recv.at[n],
                        tensor=2 * at(near, lax.rem(far + o, high)) + core,
                    ).start()
                remote(mine, mine, all_send, twins_recv.at[n], tensor=partner).start()

            @stage(i, LAGS[4])
            def _():
                n = i - LAGS[4]
                near, far, at = places(n)
                wait_for(grad_ref.at[n, pl.ds(0, wide - 1)], near_recv.at[n])
                for o in range(1, wide):
                    block = grad_ref.at[n, 2 * at(lax.rem(near + o, wide), far) + core]
                    for k in range(1, high):
                        remote(
                            block, block, relay_send, far_recv.at[n],
                            tensor=2 * at(near, lax.rem(far + k, high)) + core,
                        ).start()
                    remote(block, block, twins_send, twins_recv.at[n], tensor=partner).start()

            @stage(i, LAGS[5])
            def _():
                n = i - LAGS[5]
                near, far, at = places(n)
                wait_for(grad_ref.at[n, pl.ds(0, (high - 1) * wide)], far_recv.at[n])
                for o in range(1, high):
                    for k in range(wide):
                        block = grad_ref.at[n, 2 * at(k, lax.rem(far + o, high)) + core]
                        remote(block, block, twins_send, twins_recv.at[n], tensor=partner).start()

            @stage(i, LAGS[6])
            def _():
                n = i - LAGS[6]
                wait_for(grad_ref.at[n, pl.ds(0, chips)], twins_recv.at[n])
                part, block = n // blocks, lax.rem(n, blocks)
                grad = jnp.concatenate([grad_ref[n, s] for s in range(peers)], axis=0)
                for h in range(0, width, 512):
                    here = slice(h, min(h + 512, width))
                    acc_ref[part, :, here] += dot(grad, w_ref[block, here, :], (1, 1))

                @pl.when(n == blocks - 1)
                def _():
                    wait_for(send_ref.at[most], fwd_send)

                @pl.when(block == blocks - 1)
                def _():
                    for k in range(batch):
                        c = part * batch + k

                        @pl.loop(0, peers)
                        def _(p):
                            start = pl.multiple_of(p * share + k * rows, rows)
                            send_ref[p, c] = acc_ref[part, pl.ds(start, rows), :].astype(BF)

                        spread(send_ref, recv_ref, bwd_send.at[c], bwd_recv.at[c], c)

    def drain_forward():
        wait_for(x_ref.at[most], in_send)

    def backward():
        left_acc[...] = jnp.zeros_like(left_acc)
        right_acc[...] = jnp.zeros_like(right_acc)
        stack_ref[...] = jnp.zeros_like(stack_ref)

        @pl.loop(0, chunks)
        def _(c):
            wait_for(recv_ref.at[:, c], bwd_recv.at[c])

            @pl.loop(0, peers)
            def _(s):
                here = pl.ds(pl.multiple_of(s * each, each), each)
                rows_ref[here] = unpack(recv_ref, s, c).reshape(each, rows, order)

            @pl.loop(0, rows, unroll=4)
            def _(t):
                turned = (rows_ref[:, t, :] * slope_ref[c * rows + t].astype(F32)).astype(BF)
                right_acc[...] += dot(mixed_ref[c * rows + t], turned, (1, 1))
                cube_ref[:, t, :] = dot(right_hi, turned, (1, 0))

            unmixed = cube_ref[...].reshape(side * rows, order).astype(BF)
            left_acc[...] += dot(tall_ref[c], unmixed, (0, 0))

            @pl.when(c == chunks - 1)
            def _():
                deep = stack_ref.shape[1]
                half = side // 2
                for g in range(order // 8):
                    p, at = divmod(g * 8, deep)
                    stack_ref[p, at : at + 8, :order] = left_acc[g * 8 : (g + 1) * 8]
                for g in range(half // 8):
                    p, at = divmod(order + g * 8, deep)
                    top = right_acc[g * 8 : (g + 1) * 8]
                    low = right_acc[half + g * 8 : half + (g + 1) * 8]
                    stack_ref[p, at : at + 8, :side] = top
                    stack_ref[p, at : at + 8, side : 2 * side] = low
                terms_ref[...] = stack_ref[...].astype(BF)
                for o in range(1, peers):
                    p = lax.rem(me + o, peers)
                    remote(
                        terms_ref.at[p], shares_ref.at[o - 1], share_send, share_recv, tensor=p
                    ).start()

            wait_for(send_ref.at[most, c], bwd_send.at[c])

            @pl.loop(0, peers)
            def _(s):
                here = pl.ds(pl.multiple_of(s * each, each), each)
                unmixed = cube_ref[here].reshape(each * rows, order).astype(BF)
                pack(send_ref, s, c, dot(unmixed, left_hi, (1, 1)))

            spread(send_ref, out_ref, end_send, end_recv, c)

    def combine():
        wait_for(shares_ref.at[most], share_recv)
        total = stack_ref[me]
        for o in range(1, peers):
            total = total + shares_ref[o - 1].astype(F32)
        layers_ref[layer] = total
        mine = layers_ref.at[layer]
        others(layer, layers, lambda d: remote(
            mine, mine, layer_send, layer_recv, dp=d).start())
        wait_for(layers_ref.at[pl.ds(0, layers - 1)], layer_recv)
        total = layers_ref[0]
        for d in range(1, layers):
            total = total + layers_ref[d]
        total_ref[...] = total.astype(BF)
        pltpu.make_async_copy(total_ref, sums_ref.at[me], sum_recv).start()
        others(me, peers, lambda p: remote(
            total_ref, sums_ref.at[me], sum_send, sum_recv, tensor=p).start())

        wait_for(sums_ref, sum_recv)
        wait_for(layers_ref.at[pl.ds(0, layers - 1)], layer_send)
        wait_for(shares_ref.at[most], share_send)
        wait_for(shares_ref.at[most], sum_send)

    def drain_ends():
        wait_for(out_ref, end_recv)
        wait_for(send_ref.at[most], end_send)

    def drain_blocks():
        wait_for(part_ref.at[:, 0], pair_send)
        wait_for(got_ref, got_send)
        wait_for(last_ref, last_send)
        wait_for(grad_ref.at[:, pl.ds(0, wide + high - 1)], all_send)
        wait_for(grad_ref.at[:, pl.ds(0, (wide - 1) * (high - 1))], relay_send)
        wait_for(grad_ref.at[:, pl.ds(0, chips - 1)], twins_send)

    forward()
    project()
    drain_forward()
    backward()
    combine()
    drain_ends()
    drain_blocks()


def finish_kernel(
    grad_ref, sums_ref, out_ref, left_ref, right_ref, in_buf, out_buf, in_sem, out_sem
):
    steps = in_buf.shape[0]

    def load(i):
        return pltpu.make_async_copy(grad_ref.at[i], in_buf.at[i], in_sem.at[i])

    def store(i):
        return pltpu.make_async_copy(out_buf.at[i], out_ref.at[i], out_sem.at[i])

    for i in range(steps):
        load(i).start()
    order, side = left_ref.shape[0], right_ref.shape[0]
    half = side // 2
    left_ref[...] = sums_ref[:order, :order].astype(F32)
    right_ref[:half] = sums_ref[order : order + half, :side].astype(F32)
    right_ref[half:] = sums_ref[order : order + half, side : 2 * side].astype(F32)
    for i in range(steps):
        load(i).wait()
        out_buf[i] = in_buf[i].astype(F32)
        store(i).start()
    for i in range(steps):
        store(i).wait()


def finish(grad, sums, order, side):
    tokens, width = grad.shape
    steps = tokens // 32
    split_up = (steps, 32, width)
    hbm = pl.BlockSpec(memory_space=pl.ANY)
    vmem = pl.BlockSpec(memory_space=pltpu.VMEM)
    out, left, right = pl.pallas_call(
        finish_kernel,
        in_specs=[hbm, vmem],
        out_specs=[hbm, vmem, vmem],
        out_shape=[
            jax.ShapeDtypeStruct(split_up, F32),
            jax.ShapeDtypeStruct((order, order), F32),
            jax.ShapeDtypeStruct((side, side), F32),
        ],
        scratch_shapes=[
            pltpu.VMEM(split_up, BF),
            pltpu.VMEM(split_up, F32),
            pltpu.SemaphoreType.DMA((steps,)),
            pltpu.SemaphoreType.DMA((steps,)),
        ],
    )(grad.reshape(split_up), sums)
    return out.reshape(tokens, width), left, right


def local(activations, left_factor, right_factor, clip_scale, weight_rows, target):
    peers, layers = lax.axis_size("tensor"), lax.axis_size("dp")
    tokens, width = activations.shape
    order, side = left_factor.shape[0], right_factor.shape[0]
    out = weight_rows.shape[1]
    own = tokens // peers
    rows = min(own, 8)
    chunks = own // rows
    chips = peers // 2
    across = max(b for b in range(1, chips + 1) if chips % b == 0 and b * b <= chips)
    across = chips // across
    cols = next(b for b in (512, 256, 128) if out % b == 0)
    blocks = out // cols
    parts = 1
    steps, share = parts * blocks, own // parts
    lanes = -(-max(order, 2 * side) // 128) * 128
    deep = -(-(order + side // 2) // (8 * peers)) * 8
    flat = (peers, chunks, rows, width)
    cube = (own, side, order)
    piece = (peers, deep, lanes)
    dma = pltpu.SemaphoreType.DMA
    hbm = pl.BlockSpec(memory_space=pl.ANY)
    vmem = pl.BlockSpec(memory_space=pltpu.VMEM)
    scratch = (
        [pltpu.VMEM(flat, BF)] * 3
        + [pltpu.VMEM((chunks, side * rows, order), BF)]
        + [pltpu.VMEM(cube, BF)] * 2
        + [
            pltpu.VMEM((side, rows, order), F32),
            pltpu.VMEM((side, rows, order), F32),
            pltpu.VMEM((blocks, width, cols), BF),
            pltpu.VMEM((peers, share, width), BF),
            pltpu.VMEM((own, out), BF),
            pltpu.VMEM((steps, 2, chips, share, cols), BF),
            pltpu.VMEM((steps, chips, share, cols), BF),
            pltpu.VMEM((steps, across - 1, chips // across, share, cols), BF),
            pltpu.VMEM((steps, chips // across - 1, share, cols), BF),
            pltpu.VMEM((steps, peers, share, cols), BF),
            pltpu.VMEM((parts, tokens // parts, width), F32),
            pltpu.VMEM((order, order), F32),
            pltpu.VMEM((side, side), F32),
            pltpu.VMEM(piece, F32),
            pltpu.VMEM(piece, BF),
            pltpu.VMEM(piece, BF),
            pltpu.VMEM((layers, deep, lanes), F32),
            pltpu.VMEM((deep, lanes), BF),
        ]
        + [dma, dma((chunks,))] * 2
        + [dma((chunks,))] * 2
        + [dma] * 2
        + [dma((blocks,)), dma]
        + [dma, dma((steps,))] * 6
        + [dma] * 6
    )
    grad, sums = pl.pallas_call(
        kernel,
        out_shape=[jax.ShapeDtypeStruct(flat, BF), jax.ShapeDtypeStruct(piece, BF)],
        in_specs=[hbm, vmem, vmem, vmem, hbm, hbm],
        out_specs=[hbm, hbm],
        scratch_shapes=scratch,
        compiler_params=pltpu.CompilerParams(
            collective_id=0, has_side_effects=True, vmem_limit_bytes=67043328
        ),
    )(
        activations.reshape(flat), left_factor, right_factor, clip_scale.T,
        weight_rows, target.reshape(peers, own, out),
    )
    input_grad, left_sum, right_sum = finish(
        grad.reshape(tokens, width), sums.reshape(peers * deep, lanes), order, side
    )
    return (left_sum, right_sum, input_grad)


def solution(mesh):
    placed = (P("dp", "tensor"), P(), P(), P(), P("tensor", None), P("dp", None))
    return jax.shard_map(
        local, mesh=mesh, in_specs=placed, out_specs=(P(), P(), P("dp", "tensor")), check_vma=False
    )
```

time: 280 us -> 134 us (0.48)
  waiting for transfers between devices: 90 us -> 0 us
  Pallas kernels: 46.4 us -> 133 us
  blocking collectives: 79.9 us -> 0 us
  matrix products: 32.9 us -> 0 us
  starting transfers between devices: 16.4 us -> 0 us
  local copies, waits for them, and re-layouts: 6.86 us -> 0 us
  other arithmetic: 6.02 us -> 0 us
    pallas_call x3 -> x2, Pallas kernels: 46.4 us -> 133 us  [the longest x1 129 us: local(): pl.pallas_call(kernel, out_shape=[jax.ShapeDtypeStruct(flat, BF), jax.Sha...]
    all_to_all x4 -> x0, waiting for transfers between devices: 83.6 us -> none  [the longest x3 66.6 us: exchange(): lax.all_to_all(blocks.reshape(tok_rows, width), 'tensor', split_axis=0, c...]
    all_to_all x5 -> x0, blocking collectives: 79.9 us -> none  [the longest x1 27.4 us: exchange(): lax.all_to_all(blocks.reshape(tok_rows, width), 'tensor', split_axis=0, c...]
    dot_general x2 -> x0, matrix products: 32.9 us -> none  [the longest x1 16.5 us: local(): jnp.dot(clipped, weight_rows, preferred_element_type=F32).astype(BF)]
    all_to_all x4 -> x0, starting transfers between devices: 16.4 us -> none  [the longest x3 12.8 us: exchange(): lax.all_to_all(blocks.reshape(tok_rows, width), 'tensor', split_axis=0, c...]
    ppermute x2 -> x0, waiting for transfers between devices: 6.41 us -> none  [the longest x1 3.37 us: local(): there = lax.ppermute(there, 'tensor', swap)]
    convert_element_type x3 -> x0, other arithmetic: 5.36 us -> none  [the longest x1 2.71 us: local(): paired = (here.astype(F32) + there.astype(F32)).astype(BF)]
    unnamed x13 -> x0, local copies, waits for them, and re-layouts: 4.15 us -> none
  transfers between devices with their start and end apart: 6 -> 0, of which waited for: 6 -> 0; matrix products, arithmetic and copies ran while one was open for 1% -> 0% of each run, Pallas kernels for 0% -> 0%
where the time goes in v3:
time: 134 us
  Pallas kernels  133 us (99%)
    pallas_call x1, Pallas kernels, local(): pl.pallas_call(kernel, out_shape=[jax.ShapeDtypeStruct(flat, BF), jax.Sha...  129 us
    pallas_call x1, Pallas kernels, finish(): pl.pallas_call(finish_kernel, in_specs=[hbm, vmem], out_specs=[hbm, vmem,...  4.5 us

profile of v3, /device:TPU:0, one launch (start us, length us, event | category | flops | bytes accessed | tf_op | source)
XLA Modules:
  0.0 133.8 jit_solution(11705703687304851359)
XLA Ops:
  0.6 128.7 %shard_map.85 = (bf16[8,4,8,3456]{3,2,1,0:T(8,128)(2,1)}, bf16[8,40,256]{2,1,0:T(8,128)(2,1)}) custom-call(bf16[8,4,8,3456]{3,2,1,0:T(8,128)(2,1)} %bitcast.8, f32[216,216]{1,0:T(8,128)} %left_ref.1, f32[128,128]{1,0:T(8,128)} %right_ref.1, f32[216,128]{1,0:T(8,128)} %bitcast.10, bf16[3456,5120]{1,0:T(8,128)(2,1)} %weight_ref.1, bf16[8,32,5120]{2,1,0:T(8,128)(2,1)} %bitcast.6), custom_call_target="tpu_custom_call" | custom-call | tf_op jit(solution)/shard_map/pallas_call | solution.py:513
  129.3 4.5 %shard_map.86 = (f32[8,32,3456]{2,1,0:T(8,128)}, f32[216,216]{1,0:T(8,128)}, f32[128,128]{1,0:T(8,128)}) custom-call(bf16[8,32,3456]{2,1,0:T(8,128)(2,1)} %bitcast.7, bf16[320,256]{1,0:T(8,128)(2,1)} %bitcast.9), custom_call_target="tpu_custom_call" | custom-call | tf_op jit(solution)/shard_map/pallas_call | solution.py:440

commit v4 on v3

--- a/solution.py
+++ b/solution.py
@@ -351,6 +351,10 @@
                         terms_ref.at[p], shares_ref.at[o - 1], share_send, share_recv, tensor=p
                     ).start()
 
+                @pl.loop(1, chunks - 1)
+                def _(k):
+                    spread(send_ref, out_ref, end_send, end_recv, k)
+
             wait_for(send_ref.at[most, c], bwd_send.at[c])
 
             @pl.loop(0, peers)
@@ -359,7 +363,11 @@
                 unmixed = cube_ref[here].reshape(each * rows, order).astype(BF)
                 pack(send_ref, s, c, dot(unmixed, left_hi, (1, 1)))
 
-            spread(send_ref, out_ref, end_send, end_recv, c)
+            if chunks > 1:
+
+                @pl.when(c == 0)
+                def _():
+                    spread(send_ref, out_ref, end_send, end_recv, c)
 
     def combine():
         wait_for(shares_ref.at[most], share_recv)
@@ -378,6 +386,7 @@
         pltpu.make_async_copy(total_ref, sums_ref.at[me], sum_recv).start()
         others(me, peers, lambda p: remote(
             total_ref, sums_ref.at[me], sum_send, sum_recv, tensor=p).start())
+        spread(send_ref, out_ref, end_send, end_recv, chunks - 1)
 
         wait_for(sums_ref, sum_recv)
         wait_for(layers_ref.at[pl.ds(0, layers - 1)], layer_send)

time: 134 us -> 131 us (0.978)
  Pallas kernels: 133 us -> 130 us
    pallas_call x1, Pallas kernels: 129 us -> 125 us  [local(): pl.pallas_call(kernel, out_shape=[jax.ShapeDtypeStruct(flat, BF), jax.Sha...]
where the time goes in v4:
time: 131 us
  Pallas kernels  130 us (99%)
    pallas_call x1, Pallas kernels, local(): pl.pallas_call(kernel, out_shape=[jax.ShapeDtypeStruct(flat, BF), jax.Sha...  125 us
    pallas_call x1, Pallas kernels, finish(): pl.pallas_call(finish_kernel, in_specs=[hbm, vmem], out_specs=[hbm, vmem,...  4.5 us

profile of v4, /device:TPU:0, one launch (start us, length us, event | category | flops | bytes accessed | tf_op | source)
XLA Modules:
  0.0 130.6 jit_solution(6659439540196934898)
XLA Ops:
  0.6 125.4 %shard_map.85 = (bf16[8,4,8,3456]{3,2,1,0:T(8,128)(2,1)}, bf16[8,40,256]{2,1,0:T(8,128)(2,1)}) custom-call(bf16[8,4,8,3456]{3,2,1,0:T(8,128)(2,1)} %bitcast.8, f32[216,216]{1,0:T(8,128)} %left_ref.1, f32[128,128]{1,0:T(8,128)} %right_ref.1, f32[216,128]{1,0:T(8,128)} %bitcast.10, bf16[3456,5120]{1,0:T(8,128)(2,1)} %weight_ref.1, bf16[8,32,5120]{2,1,0:T(8,128)(2,1)} %bitcast.6), custom_call_target="tpu_custom_call" | custom-call | tf_op jit(solution)/shard_map/pallas_call | solution.py:522
  126.0 4.5 %shard_map.86 = (f32[8,32,3456]{2,1,0:T(8,128)}, f32[216,216]{1,0:T(8,128)}, f32[128,128]{1,0:T(8,128)}) custom-call(bf16[8,32,3456]{2,1,0:T(8,128)(2,1)} %bitcast.7, bf16[320,256]{1,0:T(8,128)(2,1)} %bitcast.9), custom_call_target="tpu_custom_call" | custom-call | tf_op jit(solution)/shard_map/pallas_call | solution.py:449

commit v5 on v4

--- a/solution.py
+++ b/solution.py
@@ -38,13 +38,14 @@
 
 
 def kernel(
-    act_ref, left_ref, right_ref, clip_ref, weight_ref, target_ref,
+    act_ref, left_in, right_in, clip_in, weight_ref, target_ref,
     out_ref, sums_ref,
+    left_ref, right_ref, clip_ref,
     x_ref, send_ref, recv_ref,
     tall_ref, mixed_ref, slope_ref, rows_ref, cube_ref,
     w_ref, lhs_ref, aim_ref, part_ref, pair_ref, got_ref, last_ref, grad_ref, acc_ref,
     left_acc, right_acc, stack_ref, terms_ref, shares_ref, layers_ref, total_ref,
-    in_send, in_recv, fwd_send, fwd_recv, bwd_send, bwd_recv, end_send, end_recv,
+    few_sem, in_send, in_recv, fwd_send, fwd_recv, bwd_send, bwd_recv, end_send, end_recv,
     w_sem, aim_sem, pair_send, pair_recv, got_send, got_recv, last_send, last_recv,
     all_send, near_recv, relay_send, far_recv, twins_send, twins_recv,
     share_send, share_recv, layer_send, layer_recv, sum_send, sum_recv,
@@ -101,12 +102,22 @@
     def _(c):
         spread(act_ref, x_ref, in_send, in_recv.at[c], c)
 
+    few = [
+        pltpu.make_async_copy(src, dst, few_sem.at[k])
+        for k, (src, dst) in enumerate(
+            ((left_in, left_ref), (right_in, right_ref), (clip_in, clip_ref))
+        )
+    ]
+    for copy in few:
+        copy.start()
     load_aim.start()
 
     @pl.loop(0, blocks)
     def _(n):
         load_w(n).start()
 
+    for copy in few:
+        copy.wait()
     left_hi, left_lo = split(left_ref[...])
     turned_hi, turned_lo = split(jnp.transpose(right_ref[...]))
     turned_wide = jnp.concatenate([turned_hi, turned_hi, turned_lo], axis=1)
@@ -149,6 +160,34 @@
         acc_ref[...] = jnp.zeros_like(acc_ref)
         load_aim.wait()
 
+        halves = 1 if chunks % 2 else 2
+        few, deep = chunks // halves, own // halves
+
+        def arrive(half):
+            for k in range(few):
+                c = half * few + k
+                wait_for(recv_ref.at[:, c], fwd_recv.at[c])
+
+            @pl.loop(0, peers)
+            def _(s):
+                lhs_ref[half, s] = jnp.concatenate(
+                    [recv_ref[s, half * few + k] for k in range(few)], axis=0
+                )
+
+        def multiply(n, half):
+            if half == 0:
+                load_w(n).wait()
+            lhs = jnp.concatenate([lhs_ref[half, s] for s in range(peers)], axis=0)
+            full = dot(lhs, w_ref[n], (1, 0))
+            here = slice(half * deep, (half + 1) * deep)
+            for p in range(peers):
+                part_ref[n, p % 2, p // 2, here] = full[p * deep : (p + 1) * deep].astype(BF)
+
+        for half in range(halves):
+            arrive(half)
+            if half < halves - 1:
+                pl.loop(0, blocks)(lambda n: multiply(n, half))
+
         def places(n):
             row, col = chip // across, lax.rem(chip, across)
             if across * across != chips:
@@ -168,28 +207,7 @@
             @stage(i, LAGS[0])
             def _():
                 n = i - LAGS[0]
-                part, block = n // blocks, lax.rem(n, blocks)
-
-                @pl.when(block == 0)
-                def _():
-                    for k in range(batch):
-                        c = part * batch + k
-                        wait_for(recv_ref.at[:, c], fwd_recv.at[c])
-
-                    @pl.loop(0, peers)
-                    def _(s):
-                        lhs_ref[s] = jnp.concatenate(
-                            [recv_ref[s, part * batch + k] for k in range(batch)], axis=0
-                        )
-
-                @pl.when(part == 0)
-                def _():
-                    load_w(block).wait()
-
-                lhs = jnp.concatenate([lhs_ref[s] for s in range(peers)], axis=0)
-                full = dot(lhs, w_ref[block], (1, 0))
-                for p in range(peers):
-                    part_ref[n, p % 2, p // 2] = full[p * share : (p + 1) * share].astype(BF)
+                multiply(n, halves - 1)
                 remote(
                     part_ref.at[n, 1 - core], pair_ref.at[n], pair_send, pair_recv.at[n],
                     tensor=partner,
@@ -415,7 +433,8 @@
 
 
 def finish_kernel(
-    grad_ref, sums_ref, out_ref, left_ref, right_ref, in_buf, out_buf, in_sem, out_sem
+    grad_ref, sums_ref, out_ref, left_ref, right_ref,
+    in_buf, out_buf, sums_buf, left_buf, right_buf, in_sem, out_sem, few_sem,
 ):
     steps = in_buf.shape[0]
 
@@ -427,17 +446,26 @@
 
     for i in range(steps):
         load(i).start()
-    order, side = left_ref.shape[0], right_ref.shape[0]
-    half = side // 2
-    left_ref[...] = sums_ref[:order, :order].astype(F32)
-    right_ref[:half] = sums_ref[order : order + half, :side].astype(F32)
-    right_ref[half:] = sums_ref[order : order + half, side : 2 * side].astype(F32)
+    load_sums = pltpu.make_async_copy(sums_ref, sums_buf, few_sem.at[0])
+    load_sums.start()
     for i in range(steps):
         load(i).wait()
         out_buf[i] = in_buf[i].astype(F32)
         store(i).start()
+    order, side = left_buf.shape[0], right_buf.shape[0]
+    half = side // 2
+    load_sums.wait()
+    left_buf[...] = sums_buf[:order, :order].astype(F32)
+    right_buf[:half] = sums_buf[order : order + half, :side].astype(F32)
+    right_buf[half:] = sums_buf[order : order + half, side : 2 * side].astype(F32)
+    store_left = pltpu.make_async_copy(left_buf, left_ref, few_sem.at[1])
+    store_right = pltpu.make_async_copy(right_buf, right_ref, few_sem.at[2])
+    store_left.start()
+    store_right.start()
     for i in range(steps):
         store(i).wait()
+    store_left.wait()
+    store_right.wait()
 
 
 def finish(grad, sums, order, side):
@@ -445,11 +473,10 @@
     steps = tokens // 32
     split_up = (steps, 32, width)
     hbm = pl.BlockSpec(memory_space=pl.ANY)
-    vmem = pl.BlockSpec(memory_space=pltpu.VMEM)
     out, left, right = pl.pallas_call(
         finish_kernel,
-        in_specs=[hbm, vmem],
-        out_specs=[hbm, vmem, vmem],
+        in_specs=[hbm, hbm],
+        out_specs=[hbm, hbm, hbm],
         out_shape=[
             jax.ShapeDtypeStruct(split_up, F32),
             jax.ShapeDtypeStruct((order, order), F32),
@@ -458,8 +485,12 @@
         scratch_shapes=[
             pltpu.VMEM(split_up, BF),
             pltpu.VMEM(split_up, F32),
+            pltpu.VMEM(sums.shape, BF),
+            pltpu.VMEM((order, order), F32),
+            pltpu.VMEM((side, side), F32),
             pltpu.SemaphoreType.DMA((steps,)),
             pltpu.SemaphoreType.DMA((steps,)),
+            pltpu.SemaphoreType.DMA((3,)),
         ],
     )(grad.reshape(split_up), sums)
     return out.reshape(tokens, width), left, right
@@ -478,7 +509,7 @@
     across = chips // across
     cols = next(b for b in (512, 256, 128) if out % b == 0)
     blocks = out // cols
-    parts = 1
+    parts, halves = 1, 1 if chunks % 2 else 2
     steps, share = parts * blocks, own // parts
     lanes = -(-max(order, 2 * side) // 128) * 128
     deep = -(-(order + side // 2) // (8 * peers)) * 8
@@ -487,16 +518,16 @@
     piece = (peers, deep, lanes)
     dma = pltpu.SemaphoreType.DMA
     hbm = pl.BlockSpec(memory_space=pl.ANY)
-    vmem = pl.BlockSpec(memory_space=pltpu.VMEM)
     scratch = (
-        [pltpu.VMEM(flat, BF)] * 3
+        [pltpu.VMEM((order, order), F32), pltpu.VMEM((side, side), F32), pltpu.VMEM((order, side), F32)]
+        + [pltpu.VMEM(flat, BF)] * 3
         + [pltpu.VMEM((chunks, side * rows, order), BF)]
         + [pltpu.VMEM(cube, BF)] * 2
         + [
             pltpu.VMEM((side, rows, order), F32),
             pltpu.VMEM((side, rows, order), F32),
             pltpu.VMEM((blocks, width, cols), BF),
-            pltpu.VMEM((peers, share, width), BF),
+            pltpu.VMEM((halves, peers, own // halves, width), BF),
             pltpu.VMEM((own, out), BF),
             pltpu.VMEM((steps, 2, chips, share, cols), BF),
             pltpu.VMEM((steps, chips, share, cols), BF),
@@ -512,6 +543,7 @@
             pltpu.VMEM((layers, deep, lanes), F32),
             pltpu.VMEM((deep, lanes), BF),
         ]
+        + [dma((3,))]
         + [dma, dma((chunks,))] * 2
         + [dma((chunks,))] * 2
         + [dma] * 2
@@ -522,7 +554,7 @@
     grad, sums = pl.pallas_call(
         kernel,
         out_shape=[jax.ShapeDtypeStruct(flat, BF), jax.ShapeDtypeStruct(piece, BF)],
-        in_specs=[hbm, vmem, vmem, vmem, hbm, hbm],
+        in_specs=[hbm] * 6,
         out_specs=[hbm, hbm],
         scratch_shapes=scratch,
         compiler_params=pltpu.CompilerParams(

time: 131 us -> 129 us (0.985)
  Pallas kernels: 130 us -> 128 us
    pallas_call x1, Pallas kernels: 4.5 us -> 3 us  [finish(): pl.pallas_call(finish_kernel, in_specs=[hbm, hbm], out_specs=[hbm, hbm, h...]
where the time goes in v5:
time: 129 us
  Pallas kernels  128 us (99%)
    pallas_call x1, Pallas kernels, local(): pl.pallas_call(kernel, out_shape=[jax.ShapeDtypeStruct(flat, BF), jax.Sha...  125 us
    pallas_call x1, Pallas kernels, finish(): pl.pallas_call(finish_kernel, in_specs=[hbm, hbm], out_specs=[hbm, hbm, h...  3 us

profile of v5, /device:TPU:0, one launch (start us, length us, event | category | flops | bytes accessed | tf_op | source)
XLA Modules:
  0.0 128.6 jit_solution(16457171977737080973)
XLA Ops:
  0.6 125.0 %shard_map.85 = (bf16[8,4,8,3456]{3,2,1,0:T(8,128)(2,1)}, bf16[8,40,256]{2,1,0:T(8,128)(2,1)}) custom-call(bf16[8,4,8,3456]{3,2,1,0:T(8,128)(2,1)} %bitcast.8, f32[216,216]{1,0:T(8,128)} %left_in.1, f32[128,128]{1,0:T(8,128)} %right_in.1, f32[216,128]{1,0:T(8,128)} %bitcast.10, bf16[3456,5120]{1,0:T(8,128)(2,1)} %weight_ref.1, bf16[8,32,5120]{2,1,0:T(8,128)(2,1)} %bitcast.6), custom_call_target="tpu_custom_call" | custom-call | tf_op jit(solution)/shard_map/pallas_call | solution.py:554
  125.6 3.0 %shard_map.86 = (f32[8,32,3456]{2,1,0:T(8,128)}, f32[216,216]{1,0:T(8,128)}, f32[128,128]{1,0:T(8,128)}) custom-call(bf16[8,32,3456]{2,1,0:T(8,128)(2,1)} %bitcast.7, bf16[320,256]{1,0:T(8,128)(2,1)} %bitcast.9), custom_call_target="tpu_custom_call" | custom-call | tf_op jit(solution)/shard_map/pallas_call | solution.py:476

commit v6 on v5

--- a/solution.py
+++ b/solution.py
@@ -139,7 +139,7 @@
                 for j in range(each):
                     rows_ref[s * each + j] = mixed[j * rows : (j + 1) * rows]
 
-            @pl.loop(0, rows, unroll=4)
+            @pl.loop(0, rows, unroll=8)
             def _(t):
                 mixed = rows_ref[:, t, :]
                 hi, lo = split(mixed)
@@ -340,7 +340,7 @@
                 here = pl.ds(pl.multiple_of(s * each, each), each)
                 rows_ref[here] = unpack(recv_ref, s, c).reshape(each, rows, order)
 
-            @pl.loop(0, rows, unroll=4)
+            @pl.loop(0, rows, unroll=8)
             def _(t):
                 turned = (rows_ref[:, t, :] * slope_ref[c * rows + t].astype(F32)).astype(BF)
                 right_acc[...] += dot(mixed_ref[c * rows + t], turned, (1, 1))

time: 129 us -> 129 us (level)
  no operation moved by 1% of the time
where the time goes in v6:
time: 129 us; the launch traced here: 128 us
  Pallas kernels  127 us (98%)
    pallas_call x1, Pallas kernels, local(): pl.pallas_call(kernel, out_shape=[jax.ShapeDtypeStruct(flat, BF), jax.Sha...  124 us
    pallas_call x1, Pallas kernels, finish(): pl.pallas_call(finish_kernel, in_specs=[hbm, hbm], out_specs=[hbm, hbm, h...  3 us

profile of v6, /device:TPU:0, one launch (start us, length us, event | category | flops | bytes accessed | tf_op | source)
XLA Modules:
  0.0 128.1 jit_solution(15050442120472296516)
XLA Ops:
  0.6 124.5 %shard_map.85 = (bf16[8,4,8,3456]{3,2,1,0:T(8,128)(2,1)}, bf16[8,40,256]{2,1,0:T(8,128)(2,1)}) custom-call(bf16[8,4,8,3456]{3,2,1,0:T(8,128)(2,1)} %bitcast.8, f32[216,216]{1,0:T(8,128)} %left_in.1, f32[128,128]{1,0:T(8,128)} %right_in.1, f32[216,128]{1,0:T(8,128)} %bitcast.10, bf16[3456,5120]{1,0:T(8,128)(2,1)} %weight_ref.1, bf16[8,32,5120]{2,1,0:T(8,128)(2,1)} %bitcast.6), custom_call_target="tpu_custom_call" | custom-call | tf_op jit(solution)/shard_map/pallas_call | solution.py:554
  125.1 3.0 %shard_map.86 = (f32[8,32,3456]{2,1,0:T(8,128)}, f32[216,216]{1,0:T(8,128)}, f32[128,128]{1,0:T(8,128)}) custom-call(bf16[8,32,3456]{2,1,0:T(8,128)(2,1)} %bitcast.7, bf16[320,256]{1,0:T(8,128)(2,1)} %bitcast.9), custom_call_target="tpu_custom_call" | custom-call | tf_op jit(solution)/shard_map/pallas_call | solution.py:476
